TPU v7x, 32 devices: a whole 2x2x4 slice. The times are simulated.
32 devices in a mesh: head: 8 (over z, x), client: 4 (over y, core).
Axes of the slice: x: 2, y: 2, z: 4, core: 2. Of those that a mesh axis runs over, the one named last changes fastest.
Arguments:
- client_ids: int32 [32], replicated, may hold values from 0 to 127, as said below
- client_table: bfloat16 [128, 256], replicated, may hold values from -6 to 6
- in_weight: bfloat16 [256, 4096], P(None, 'client'), may hold values from -0.375 to 0.375
- in_bias: float32 [4096], P('client'), may hold values from -3 to 3
- head_weight: bfloat16 [4096, 131072], P('client', 'head'), may hold values from -0.09375 to 0.09375
- tokens: int32 [32, 256], P(('head', 'client')), may hold values from 0 to 255
- labels: int32 [32, 256], P(('head', 'client')), may hold values from 0 to 255
- byte_table: bfloat16 [256, 4096], P(None, 'client'), may hold values from -5.5 to 6.7
- out_table: bfloat16 [256, 4096], P(None, 'client'), may hold values from -5.625 to 5.625
Outputs:
- head_grad: bfloat16 [4096, 131072], P('client', 'head')
- in_grad: float32 [256, 4096], P(None, 'client')
- losses: float32 [32], P(('head', 'client'))
Inputs may be any that keep to these rules, and one draw needn't show every extreme that they name: `client_ids`: distinct population indices.
All inputs are finite; a program needn't handle non-finite values.
Results may differ from a plain program's by a relative error of at most 0.0085.
Values may be sent and summed in bfloat16 or wider, within the bound.
A program may use at most 128 MiB of HBM per device.

v0:
```python
import jax
import jax.numpy as jnp
from jax import lax
from jax.sharding import PartitionSpec as P

EPSILON = 1e-06
learn_rate = 0.1


FULL = lax.Precision.HIGHEST


def mm(x, y, over_x=1, over_y=0):
    return lax.dot_general(
        x, y, (((over_x,), (over_y,)), ((), ())), precision=FULL, preferred_element_type=jnp.float32
    )


def exact(x, y, over_x, over_y):
    return lax.dot_general(
        x, y, (((over_x,), (over_y,)), ((), ())), preferred_element_type=jnp.float32
    )


def halves(x):
    top = lax.reduce_precision(x, 8, 7)
    rest = x - top
    return jnp.concatenate([top.astype(jnp.bfloat16), rest.astype(jnp.bfloat16)], 1)


def inner_step(u, n_in, m_out, k_bb, gram_io, mean_in, pair_count, depth, scale):
    uk = mm(u, k_bb)
    z = gram_io + scale * mm(u, m_out, 1, 1)
    q = mean_in + jnp.sum(u * (2.0 * scale * n_in + (scale * scale) * uk), -1, keepdims=True) / depth
    r = lax.rsqrt(q + EPSILON)
    kappa = 4.0 / jnp.sqrt(jnp.float32(depth))
    logits = (kappa * r) * z
    top = jnp.max(logits, -1, keepdims=True)
    raised = jnp.exp(logits - top)
    total = jnp.sum(raised, -1, keepdims=True)
    row_count = jnp.sum(pair_count, -1, keepdims=True)
    loss = jnp.sum(row_count * (jnp.log(total) + top)) - jnp.sum(pair_count * logits)
    slope = row_count * (raised / total) - pair_count
    dz = (kappa * r) * slope
    dr = kappa * jnp.sum(slope * z, -1, keepdims=True)
    e = dr * (-1.0 / depth) * (r * r * r)
    gu = scale * (mm(dz, m_out) + e * (n_in + scale * uk))
    w = mm(dz, u, 0, 0)
    x = e * u
    y = mm(u, x, 0, 0)
    return loss, gu, w, x, y


def table_products(byte_full, out_full):
    depth = byte_full.shape[1]
    gram_ii = exact(byte_full, byte_full, 1, 1)
    gram_io = exact(byte_full, out_full, 1, 1)
    gram_oo = exact(out_full, out_full, 1, 1)
    size = gram_ii.shape[0]
    diagonal = lax.broadcasted_iota(jnp.int32, (size, size), 0) == lax.broadcasted_iota(
        jnp.int32, (size, size), 1
    )
    mean_in = jnp.sum(jnp.where(diagonal, gram_ii, 0.0), -1, keepdims=True) / depth
    return gram_ii, gram_io, gram_oo, mean_in


def train_client(factor_row, token_row, label_row, byte_full, out_full, products):
    gram_ii, gram_io, gram_oo, mean_in = products
    vocab, depth = byte_full.shape
    split_at = factor_row.shape[0] // 2
    rank = split_at // depth
    scale = 1.0 / jnp.sqrt(jnp.float32(depth * rank))
    a0 = factor_row[:split_at].reshape(depth, rank)
    b0 = factor_row[split_at:].reshape(rank, depth)
    ids = lax.broadcasted_iota(jnp.int32, (vocab, token_row.shape[0]), 0)
    pair_count = exact(
        (ids == token_row[None, :]).astype(jnp.bfloat16),
        (ids == label_row[None, :]).astype(jnp.bfloat16),
        1,
        1,
    )
    rn = lax.rsqrt(mean_in + EPSILON)
    u0 = rn * exact(byte_full, a0, 1, 0)
    n0 = exact(byte_full, b0, 1, 1)
    m0 = exact(out_full, b0, 1, 1)
    k0 = exact(b0, b0, 1, 1)
    fixed = (gram_io, mean_in, pair_count, depth, scale)
    first_loss, gu0, w0, x0, y0 = inner_step(u0, n0, m0, k0, *fixed)
    rate = learn_rate * scale
    w0, x0, y0 = -rate * w0, -rate * x0, (-rate * scale) * y0
    u1 = u0 - learn_rate * rn * mm(gram_ii, rn * gu0)
    n1 = n0 + mm(gram_io, w0) + mm(gram_ii, x0) + mm(n0, y0)
    m1 = m0 + mm(gram_oo, w0) + mm(gram_io, x0, 0, 0) + mm(m0, y0)
    cross = k0 + mm(y0, k0, 0, 0) + mm(w0, m0, 0, 0) + mm(x0, n0, 0, 0)
    k1 = cross + mm(cross, y0) + mm(m1, w0, 0, 0) + mm(n1, x0, 0, 0)
    _, gu1, w1, x1, y1 = inner_step(u1, n1, m1, k1, *fixed)
    w1, x1, y1 = -rate * w1, -rate * x1, (-rate * scale) * y1
    ga = (-learn_rate) * rn * (gu0 + gu1)
    wf = w0 + w1 + mm(w0, y1)
    xf = x0 + x1 + mm(x0, y1)
    yf = y0 + y1 + mm(y0, y1)
    da = exact(byte_full, halves(ga), 0, 0)
    da = da[:, :rank] + da[:, rank:]
    db = (
        exact(halves(wf), out_full, 0, 0)
        + exact(halves(xf), byte_full, 0, 0)
        + exact(halves(yf), b0, 0, 0)
    )
    db = db[:rank] + db[rank:]
    deltas = jnp.concatenate([da.astype(jnp.bfloat16).reshape(-1), db.astype(jnp.bfloat16).reshape(-1)])
    return deltas, first_loss / token_row.shape[0]


def local(
    client_ids, client_table, in_weight, in_bias, head_weight, tokens, labels, byte_table, out_table
):
    head_count = lax.axis_size("head")
    group_count = lax.axis_size("client")
    per_device = tokens.shape[0]
    byte_full, out_full = (
        lax.all_gather(byte_table, "client", axis=1, tiled=True),
        lax.all_gather(out_table, "client", axis=1, tiled=True),
    )
    products = table_products(byte_full, out_full)
    ordered = client_ids.reshape(head_count, group_count, per_device).transpose(1, 0, 2).reshape(-1)
    chosen = client_table[ordered]
    preact = jnp.dot(chosen, in_weight, preferred_element_type=jnp.float32) + in_bias
    hidden = jnp.maximum(preact, 0.0).astype(jnp.bfloat16)
    partial = jnp.dot(hidden, head_weight, preferred_element_type=jnp.float32).astype(jnp.bfloat16)
    rows, columns = partial.shape
    parts = lax.all_to_all(
        partial.reshape(group_count, rows // group_count, columns), "client", split_axis=0, concat_axis=0
    )
    summed = jnp.sum(parts.astype(jnp.float32), 0)
    owned = lax.all_to_all(
        summed.astype(jnp.bfloat16), "head", split_axis=0, concat_axis=1, tiled=True
    )
    trained = [
        train_client(owned[i], tokens[i], labels[i], byte_full, out_full, products)
        for i in range(per_device)
    ]
    deltas = jnp.stack([t[0] for t in trained])
    losses = jnp.stack([t[1] for t in trained])
    returned = lax.all_to_all(deltas, "head", split_axis=1, concat_axis=0, tiled=True)
    received = lax.all_gather(returned, "client", axis=0, tiled=True)
    back = lax.dot_general(
        received, head_weight, (((1,), (1,)), ((), ())), preferred_element_type=jnp.float32
    )
    back = lax.all_to_all(
        back.reshape(head_count, rows // head_count, back.shape[1]), "head", split_axis=0, concat_axis=0
    )
    back = jnp.sum(back, 0)
    back = lax.all_to_all(
        jnp.broadcast_to(back[None], (head_count,) + back.shape), "head", split_axis=0, concat_axis=0
    )
    hidden_back = back.reshape(rows, back.shape[2])
    grad_sum = lax.dot_general(
        hidden, received, (((0,), (0,)), ((), ())), preferred_element_type=jnp.float32
    )
    masked = jnp.where(preact > 0, hidden_back, 0.0)
    in_grad = lax.dot_general(
        chosen.astype(jnp.float32),
        masked,
        (((0,), (0,)), ((), ())),
        precision=FULL,
    )
    return (grad_sum.astype(jnp.bfloat16), in_grad, losses)


def solution(mesh):
    placed = (
        P(),
        P(),
        P(None, "client"),
        P("client"),
        P("client", "head"),
        P(("head", "client"), None),
        P(("head", "client"), None),
        P(None, "client"),
        P(None, "client"),
    )
    return jax.shard_map(
        local,
        mesh=mesh,
        in_specs=placed,
        out_specs=(P("client", "head"), P(None, "client"), P(("head", "client"))),
        check_vma=False,
    )
```

profile of v0, /device:TPU:0, one launch (start us, length us, event | category | flops | bytes accessed | tf_op | source)
XLA Modules:
  0.0 178.3 jit_solution(9570034128305382176)
XLA Ops:
  8.8 1.5 gather_fusion
  10.3 0.9 convolution_add_fusion.2
  11.2 15.3 %fusion = bf16[4,8,16384]{2,1,0:T(8,128)(2,1)} fusion(bf16[1024,16384]{1,0:T(8,128)(2,1)} %param.13, f32[32,1024]{1,0:T(8,128)S(1)} %convolution_add_fusion.2), kind=kOutput, calls=%fused_computation.3 | convolution fusion | flops 1074331648 | bytes 34734080 | tf_op jit(solution)/shard_map/dot_general | solution.py:129
  26.5 4.3 %all-to-all-start = ((bf16[4,8,16384]{2,1,0:T(8,128)(2,1)}), bf16[4,8,16384]{2,1,0:T(8,128)(2,1)S(1)}, u32[]{:S(2)}, u32[]{:S(2)}) async-start(bf16[4,8,16384]{2,1,0:T(8,128)(2,1)} %fusion), calls=%async_computation | async-start | bytes 2097152 | tf_op jit(solution)/shard_map/all_to_all | solution.py:131
  31.6 13.6 %all-to-all-done = bf16[4,8,16384]{2,1,0:T(8,128)(2,1)S(1)} async-done(((bf16[4,8,16384]{2,1,0:T(8,128)(2,1)}), bf16[4,8,16384]{2,1,0:T(8,128)(2,1)S(1)}, u32[]{:S(2)}, u32[]{:S(2)}) %all-to-all-start) | async-done | bytes 1048608 | tf_op jit(solution)/shard_map/all_to_all | solution.py:131
  47.0 14.9 %all_to_all.45 = bf16[8,2,8192]{2,1,0:T(2,128)(2,1)S(1)} all-to-all(bf16[8,2,8192]{2,1,0:T(2,128)(2,1)S(1)} %reshape.188), channel_id=1, replica_groups=mesh['head'=8,'client'=4] {'head'}, dimensions={0} | all-to-all | bytes 524288 | tf_op jit(solution)/shard_map/all_to_all | solution.py:135
  62.2 1.2 slice_reduce_fusion
  63.4 1.7 reshape.171
  65.4 3.1 %select_reduce_fusion = (f32[256]{0:T(256)S(1)}, f32[256,256]{0,1:T(8,128)S(1)}) fusion(bf16[256,4096]{1,0:T(8,128)(2,1)} %all-gather.5.cloned.1.call-done), kind=kOutput, calls=%fused_computation.58 | convolution fusion | flops 537067264 | bytes 2360320 | tf_op jit(solution)/shard_map/dot_general | solution.py:20
  70.2 2.4 %fusion.97 = f32[16,256]{1,0:T(8,128)S(1)} fusion(bf16[16,4096]{1,0:T(8,128)(2,1)S(1)} %reshape.172, bf16[256,4096]{1,0:T(8,128)(2,1)} %all-gather.7.cloned.1.call-done), kind=kOutput, calls=%fused_computation.165 | convolution fusion | flops 33554432 | bytes 2244608 | tf_op jit(solution)/shard_map/dot_general | solution.py:20
  73.8 0.9 multiply_reduce_fusion
  81.5 1.3 copy.19
  82.9 2.0 %reshape.173 = bf16[65536]{0:T(1024)(128)(2,1)S(1)} reshape(bf16[4096,16]{1,0:T(8,128)(2,1)} %copy.19) | data formatting | bytes 262144 | tf_op jit(solution)/shard_map/reshape | solution.py:110
  85.1 2.1 %fusion.42 = f32[32,4096]{1,0:T(8,128)S(1)} fusion(bf16[256,4096]{1,0:T(8,128)(2,1)} %all-gather.7.cloned.1.call-done, bf16[256,16]{0,1:T(8,128)(2,1)S(1)} %get-tuple-element.17, bf16[256,16]{0,1:T(8,128)(2,1)S(1)} %get-tuple-element.16), kind=kOutput, calls=%fused_computation.96 | convolution fusion | flops 67141632 | bytes 2637824 | tf_op jit(solution)/shard_map/dot_general | solution.py:20
  88.4 2.2 %reduce.7 = bf16[8,16384]{1,0:T(8,128)(2,1)S(1)} reduce(bf16[8,1,16384]{2,1,0:T(2,128)(2,1)S(1)} %bitcast.120, bf16[]{:T(256)} %broadcast.252), dimensions={1}, to_apply=%bitcast.52.reduce_sub_computation | reduce | bytes 524290
  90.8 11.9 %all_to_all.46 = bf16[8,2,8192]{2,1,0:T(2,128)(2,1)S(1)} all-to-all(bf16[8,2,8192]{2,1,0:T(2,128)(2,1)S(1)} %reshape.190), channel_id=1, replica_groups=mesh['head'=8,'client'=4] {'head'}, dimensions={0} | all-to-all | bytes 524288 | tf_op jit(solution)/shard_map/all_to_all | solution.py:144
  103.0 1.0 copy.21
  104.0 15.2 %all-gather.9.cloned.1.call-done = bf16[1,32,16384]{2,1,0:T(8,128)(2,1)} async-done(((bf16[1,8,16384]{2,1,0:T(8,128)(2,1)}), bf16[1,32,16384]{2,1,0:T(8,128)(2,1)}) %all-gather.9.cloned.1.call-update) | async-done | bytes 1048592 | tf_op jit(solution)/shard_map/all_gather | solution.py:145
  119.2 17.2 %fusion.11 = f32[32,1024]{1,0:T(8,128)S(1)} fusion(bf16[1024,16384]{1,0:T(8,128)(2,1)} %param.13, bf16[1,32,16384]{2,1,0:T(8,128)(2,1)} %all-gather.9.cloned.1.call-done), kind=kOutput, calls=%fused_computation.39 | convolution fusion | flops 1073741824 | bytes 34734080 | tf_op jit(solution)/shard_map/dot_general | solution.py:146
  137.1 5.5 %all-to-all-start.3 = ((f32[8,4,1024]{2,1,0:T(4,128)}), f32[8,4,1024]{2,1,0:T(4,128)S(1)}, u32[]{:S(2)}, u32[]{:S(2)}) async-start(f32[8,4,1024]{2,1,0:T(4,128)} %reshape.175), calls=%async_computation.3 | async-start | bytes 262144 | tf_op jit(solution)/shard_map/all_to_all | solution.py:149
  144.6 5.5 %all-to-all-done.3 = f32[8,4,1024]{2,1,0:T(4,128)S(1)} async-done(((f32[8,4,1024]{2,1,0:T(4,128)}), f32[8,4,1024]{2,1,0:T(4,128)S(1)}, u32[]{:S(2)}, u32[]{:S(2)}) %all-to-all-start.3) | async-done | bytes 131104 | tf_op jit(solution)/shard_map/all_to_all | solution.py:149
  150.7 3.4 %all-to-all-start.4 = ((f32[8,4,1024]{2,1,0:T(4,128)}), f32[8,4,1024]{2,1,0:T(4,128)S(1)}, u32[]{:S(2)}, u32[]{:S(2)}) async-start(f32[8,4,1024]{2,1,0:T(4,128)} %broadcast_in_dim.8), calls=%async_computation.4 | async-start | bytes 262144 | tf_op jit(solution)/shard_map/all_to_all | solution.py:153
  154.1 14.9 %convolution_convert_fusion = bf16[1024,16384]{1,0:T(8,128)(2,1)} fusion(bf16[1,32,16384]{2,1,0:T(8,128)(2,1)S(1)} %copy-done.4, f32[32,1024]{1,0:T(8,128)S(1)} %convolution_add_fusion.2), kind=kOutput, calls=%fused_computation.1 | convolution fusion | flops 1090584576 | bytes 34734080 | tf_op jit(solution)/shard_map/dot_general | solution.py:157
  169.1 1.6 fusion.24
  (90 shorter events, 18.2 us)
Async XLA Ops:
  7.2 3.1 %copy-start = (bf16[256,1024]{1,0:T(8,128)(2,1)S(1)}, bf16[256,1024]{1,0:T(8,128)(2,1)}, u32[]{:S(2)}) copy-start(bf16[256,1024]{1,0:T(8,128)(2,1)} %param.11) | copy-start | bytes 1572868
  7.2 58.2 %all-gather.5.cloned.1.call-start = ((), (), s32[]{:S(2)}) async-start(), calls=%async_computation.5 | async-start | bytes 2621440 | tf_op jit(solution)/shard_map/all_gather | solution.py:121
  26.5 18.7 %all-to-all-start = ((bf16[4,8,16384]{2,1,0:T(8,128)(2,1)}), bf16[4,8,16384]{2,1,0:T(8,128)(2,1)S(1)}, u32[]{:S(2)}, u32[]{:S(2)}) async-start(bf16[4,8,16384]{2,1,0:T(8,128)(2,1)} %fusion), calls=%async_computation | async-start | bytes 2097152 | tf_op jit(solution)/shard_map/all_to_all | solution.py:131
  30.8 39.4 %all-gather.7.cloned.1.call-start = ((), (), s32[]{:S(2)}) async-start(), calls=%async_computation.6 | async-start | bytes 2621440 | tf_op jit(solution)/shard_map/all_gather | solution.py:122
  31.5 87.7 %all-gather.9.cloned.1.call-start = ((), (), s32[]{:S(2)}) async-start(), calls=%async_computation.7 | async-start | bytes 1310720 | tf_op jit(solution)/shard_map/all_gather | solution.py:145
  65.3 3.2 %copy-start.2 = (bf16[256,4096]{1,0:T(8,128)(2,1)S(1)}, bf16[256,4096]{1,0:T(8,128)(2,1)}, u32[]{:S(2)}) copy-start(bf16[256,4096]{1,0:T(8,128)(2,1)} %all-gather.5.cloned.1.call-done) | copy-start | bytes 6291460
  65.3 3.2 %copy-start.5 = (bf16[4096,16]{1,0:T(8,128)(2,1)S(1)}, bf16[4096,16]{1,0:T(8,128)(2,1)}, u32[]{:S(2)}) copy-start(bf16[4096,16]{1,0:T(8,128)(2,1)} %reshape.171) | copy-start | bytes 393220
  70.1 2.4 %copy-start.3 = (bf16[256,4096]{1,0:T(8,128)(2,1)S(1)}, bf16[256,4096]{1,0:T(8,128)(2,1)}, u32[]{:S(2)}) copy-start(bf16[256,4096]{1,0:T(8,128)(2,1)} %all-gather.7.cloned.1.call-done) | copy-start | bytes 6291460
  72.5 1.2 copy-start.6
  72.6 1.2 copy-start.7
  119.2 34.9 %copy-start.4 = (bf16[1,32,16384]{2,1,0:T(8,128)(2,1)S(1)}, bf16[1,32,16384]{2,1,0:T(8,128)(2,1)}, u32[]{:S(2)}) copy-start(bf16[1,32,16384]{2,1,0:T(8,128)(2,1)} %all-gather.9.cloned.1.call-done) | copy-start | bytes 3145732
  137.1 12.9 %all-to-all-start.3 = ((f32[8,4,1024]{2,1,0:T(4,128)}), f32[8,4,1024]{2,1,0:T(4,128)S(1)}, u32[]{:S(2)}, u32[]{:S(2)}) async-start(f32[8,4,1024]{2,1,0:T(4,128)} %reshape.175), calls=%async_computation.3 | async-start | bytes 262144 | tf_op jit(solution)/shard_map/all_to_all | solution.py:149
  150.7 18.3 %all-to-all-start.4 = ((f32[8,4,1024]{2,1,0:T(4,128)}), f32[8,4,1024]{2,1,0:T(4,128)S(1)}, u32[]{:S(2)}, u32[]{:S(2)}) async-start(f32[8,4,1024]{2,1,0:T(4,128)} %broadcast_in_dim.8), calls=%async_computation.4 | async-start | bytes 262144 | tf_op jit(solution)/shard_map/all_to_all | solution.py:153
  154.1 16.5 %copy-start.1 = (bf16[256,1024]{1,0:T(8,128)(2,1)S(1)}, bf16[256,1024]{1,0:T(8,128)(2,1)}, u32[]{:S(2)}) copy-start(bf16[256,1024]{1,0:T(8,128)(2,1)} %param.11) | copy-start | bytes 1572868
Sparse Core Ops, SparseCore 0:
  9.5 25.2 all-gather.4
  36.4 22.5 all-gather.6
  104.2 15.0 all-gather.8
where the time goes:
time: 179 us; the launch traced here: 178 us
  matrix products  68.6 us (38%)
  waiting for transfers between devices  35.7 us (20%)
  blocking collectives  26.8 us (15%)
  between operations  16.6 us (9%)
  starting transfers between devices  13.2 us (7%)
  local copies, waits for them, and re-layouts  13 us (7%)
  other arithmetic  4.36 us (2%)
    dot_general x1, matrix products, local(): lax.dot_general(received, head_weight, (((1,), (1,)), ((), ())), preferre...  17.2 us
    dot_general x1, matrix products, local(): jnp.dot(hidden, head_weight, preferred_element_type=jnp.float32)  15.3 us
    all_gather x1, waiting for transfers between devices, local(): received = lax.all_gather(returned, 'client', axis=0, tiled=True)  15.2 us
    all_to_all x1, blocking collectives, local(): lax.all_to_all(summed.astype(jnp.bfloat16), 'head', split_axis=0, concat_...  14.9 us
    dot_general x1, matrix products, local(): lax.dot_general(hidden, received, (((0,), (0,)), ((), ())), preferred_ele...  14.9 us
    all_to_all x1, waiting for transfers between devices, local(): lax.all_to_all(partial.reshape(group_count, rows // group_count, columns)...  13.6 us
    dot_general x12, matrix products, exact(): lax.dot_general(x, y, (((over_x,), (over_y,)), ((), ())), preferred_eleme...  12.7 us
    all_to_all x1, blocking collectives, local(): lax.all_to_all(deltas, 'head', split_axis=1, concat_axis=0, tiled=True)  11.9 us
  transfers between devices with their start and end apart: 6, of which 3 were waited for; matrix products, arithmetic and copies ran while one was open for 25% of the time, Pallas kernels for 0%

commit v1 on v0

--- a/solution.py
+++ b/solution.py
@@ -1,13 +1,21 @@
+import functools
+
 import jax
 import jax.numpy as jnp
 from jax import lax
+from jax.experimental import pallas as pl
+from jax.experimental.pallas import tpu as pltpu
 from jax.sharding import PartitionSpec as P
 
 EPSILON = 1e-06
 learn_rate = 0.1
-
-
 FULL = lax.Precision.HIGHEST
+LANES = 128
+PIECE_ROWS = 16
+TABLE_PIECES = 8
+HIGH_VMEM = 62 * 1024 * 1024
+F32 = jnp.float32
+BF16 = jnp.bfloat16
 
 
 def mm(x, y, over_x=1, over_y=0):
@@ -111,60 +119,597 @@
     return deltas, first_loss / token_row.shape[0]
 
 
+def to_head(h):
+    return {"head": h}
+
+
+def to_client(g):
+    return {"client": g}
+
+
+def remote(src, dst, send, recv, device):
+    return pltpu.make_async_remote_copy(
+        src_ref=src,
+        dst_ref=dst,
+        send_sem=send,
+        recv_sem=recv,
+        device_id=device,
+        device_id_type=pl.DeviceIdType.MESH,
+    )
+
+
+def meet(heads, h, g):
+    sem = pltpu.get_barrier_semaphore()
+
+    @pl.loop(1, heads)
+    def _(i):
+        pl.semaphore_signal(
+            sem, inc=1, device_id=to_head(lax.rem(h + i, heads)), device_id_type=pl.DeviceIdType.MESH
+        )
+
+    for other in (g ^ 1, g ^ 2):
+        pl.semaphore_signal(
+            sem, inc=1, device_id=to_client(other), device_id_type=pl.DeviceIdType.MESH
+        )
+    pl.semaphore_wait(sem, heads + 1)
+
+
+def forward_kernel(
+    heads, steps, ids, client_table, in_weight, in_bias, head_weight, byte_table, out_table,
+    factors, tables, hidden_out, preact_out, chosen_out,
+    wv, ct, iw, ib, tv, chosen_v, preact_v, hidden_v, s1, r1, k2, s2, r2, s3,
+    w_sem, in_sem, out_sem, own_sem, p_send, p_recv, y_send, y_recv, f_send, f_recv,
+    t_own_send, t_own_recv, t_send, t_recv, t_pair_send, t_pair_recv, tl_sem,
+):
+    h, g = lax.axis_index("head"), lax.axis_index("client")
+    core, far = g & 1, g >> 1
+    pair, peer = g ^ 1, g ^ 2
+    x_side, z_side = h ^ 1, h ^ 2
+    clients = hidden_v.shape[0]
+    group = clients // 4
+    block_rows = steps * PIECE_ROWS
+    width = PIECE_ROWS * LANES
+    vocab = tv.shape[1]
+    part = vocab // 4 // (TABLE_PIECES // 2)
+
+    small = [
+        pltpu.make_async_copy(client_table, ct, in_sem.at[0]),
+        pltpu.make_async_copy(in_weight, iw, in_sem.at[1]),
+        pltpu.make_async_copy(in_bias, ib, in_sem.at[2]),
+        pltpu.make_async_copy(byte_table, tv.at[0], in_sem.at[3]),
+        pltpu.make_async_copy(out_table, tv.at[1], in_sem.at[4]),
+    ]
+    for c in small:
+        c.start()
+
+    def w_copy(k):
+        return pltpu.make_async_copy(
+            head_weight.at[:, pl.ds(pl.multiple_of(k * width, width), width)], wv.at[k], w_sem.at[k]
+        )
+
+    @pl.loop(0, steps)
+    def _(k):
+        w_copy(k).start()
+
+    for c in small:
+        c.wait()
+    population = lax.broadcasted_iota(jnp.int32, (clients, ct.shape[0]), 1)
+    onehot = jnp.where(ids[...] == population, 1.0, 0.0).astype(BF16)
+    chosen = jnp.dot(onehot, ct[...], preferred_element_type=F32).astype(BF16)
+    chosen_v[...] = chosen
+    preact = jnp.dot(chosen, iw[...], preferred_element_type=F32) + ib[...]
+    preact_v[...] = preact
+    hidden_v[...] = jnp.maximum(preact, 0.0).astype(BF16)
+
+    meet(heads, h, g)
+
+    quarter = [tables.at[t, g] for t in range(2)]
+
+    def piece(t, owner_head, col):
+        table = lax.div(t, TABLE_PIECES // 2)
+        row = lax.rem(owner_head, 4) * (vocab // 4) + lax.rem(t, TABLE_PIECES // 2) * part
+        return table, col, pl.ds(pl.multiple_of(row, part), part)
+
+    own_to_out = [
+        pltpu.make_async_copy(tv.at[t], quarter[t], tl_sem.at[t]) for t in range(2)
+    ]
+    own_to_pair = [
+        remote(tv.at[t], quarter[t], t_own_send.at[t], t_own_recv.at[t], to_client(pair))
+        for t in range(2)
+    ]
+    for c in own_to_out + own_to_pair:
+        c.start()
+
+    def t_peer(t):
+        table, col, rows = piece(t, h, g)
+        return remote(
+            tv.at[table, rows], tables.at[table, col, rows],
+            t_send.at[0, t], t_recv.at[0, t], to_client(peer),
+        )
+
+    def t_side(kind, t):
+        table, col, rows = piece(t, h, peer)
+        ref = tables.at[table, col, rows]
+        return remote(ref, ref, t_send.at[kind, t], t_recv.at[kind, t], to_head((x_side, z_side)[kind - 1]))
+
+    def t_relay(t, odd):
+        table, col, rows = piece(t, x_side if odd else z_side, peer)
+        ref = tables.at[table, col, rows]
+        return remote(ref, ref, t_send.at[3, t], t_recv.at[3, t], to_head(z_side if odd else x_side))
+
+    def t_pair(kind, t):
+        owner = (h, x_side, z_side, h ^ 3)[kind]
+        table, col, rows = piece(t, owner, peer)
+        ref = tables.at[table, col, rows]
+        return remote(ref, ref, t_pair_send.at[kind, t], t_pair_recv.at[kind, t], to_client(pair))
+
+    def to_pair(k):
+        return remote(
+            s1.at[k, pl.ds((1 - core) * 2 * group, 2 * group)], r1.at[k],
+            p_send.at[k], p_recv.at[k], to_client(pair),
+        )
+
+    def to_peer(k):
+        return remote(s2.at[k], r2.at[k], y_send.at[k], y_recv.at[k], to_client(peer))
+
+    def rows_of(head, k):
+        return pl.ds(pl.multiple_of(head * block_rows + k * PIECE_ROWS, PIECE_ROWS), PIECE_ROWS)
+
+    def to_owner(k, i):
+        other = lax.rem(h + i, heads)
+        return remote(
+            s3.at[k, other], factors.at[rows_of(h, k)],
+            f_send.at[k, other], f_recv.at[k, h], to_head(other),
+        )
+
+    def from_owner(k, i):
+        other = lax.rem(h + i, heads)
+        return remote(
+            s3.at[k, other], factors.at[rows_of(other, k)],
+            f_send.at[k, other], f_recv.at[k, other], to_head(other),
+        )
+
+    def own_piece(k):
+        return pltpu.make_async_copy(s3.at[k, h], factors.at[rows_of(h, k)], own_sem.at[k])
+
+    small_out = [
+        pltpu.make_async_copy(hidden_v, hidden_out, out_sem.at[0]),
+        pltpu.make_async_copy(preact_v, preact_out, out_sem.at[1]),
+        pltpu.make_async_copy(chosen_v, chosen_out, out_sem.at[2]),
+    ]
+    for c in small_out:
+        c.start()
+
+    def fwd_stage(k):
+        w_copy(k).wait()
+        for n in range(width // 512):
+            out = jnp.dot(
+                hidden_v[...], wv[k, :, n * 512 : (n + 1) * 512], preferred_element_type=F32
+            )
+            for q in range(4):
+                s1[k, :, n * 4 + q, :] = out[:, q * LANES : (q + 1) * LANES]
+        to_pair(k).start()
+
+    def pair_stage(k):
+        to_pair(k).wait_recv()
+        theirs = core * 2 * group + (1 - far) * group
+        mine = core * 2 * group + far * group
+        s2[k] = (s1[k, pl.ds(theirs, group)] + r1[k, pl.ds((1 - far) * group, group)]).astype(BF16)
+        to_peer(k).start()
+        k2[k] = s1[k, pl.ds(mine, group)] + r1[k, pl.ds(far * group, group)]
+
+    def peer_stage(k):
+        to_peer(k).wait_recv()
+        s3[k] = (k2[k] + r2[k].astype(F32)).astype(BF16)
+        own_piece(k).start()
+
+        @pl.loop(1, heads)
+        def _(i):
+            to_owner(k, i).start()
+
+    def table_stage(k):
+        @pl.when(k < TABLE_PIECES // 2)
+        def _():
+            t_peer(2 * k).start()
+            t_peer(2 * k + 1).start()
+
+        for lag in range(2):
+            t0 = k - 3 - lag
+
+        @pl.when((k >= 3) & (k < 3 + TABLE_PIECES))
+        def _():
+            t = k - 3
+            t_peer(t).wait_recv()
+            t_side(1, t).start()
+            t_side(2, t).start()
+            t_pair(0, t).start()
+
+        @pl.when((k >= 5) & (k < 5 + TABLE_PIECES))
+        def _():
+            t = k - 5
+            t_side(1, t).wait_recv()
+            t_side(2, t).wait_recv()
+
+            @pl.when(lax.rem(t, 2) == 1)
+            def _():
+                t_relay(t, True).start()
+
+            @pl.when(lax.rem(t, 2) == 0)
+            def _():
+                t_relay(t, False).start()
+
+            t_pair(1, t).start()
+            t_pair(2, t).start()
+
+        @pl.when((k >= 7) & (k < 7 + TABLE_PIECES))
+        def _():
+            t = k - 7
+            t_relay(t, False).wait_recv()
+            t_pair(3, t).start()
+
+    @pl.loop(0, max(steps + 3, TABLE_PIECES + 7))
+    def _(k):
+        @pl.when(k < steps)
+        def _():
+            fwd_stage(k)
+
+        @pl.when((k >= 1) & (k < steps + 1))
+        def _():
+            pair_stage(k - 1)
+
+        @pl.when((k >= 3) & (k < steps + 3))
+        def _():
+            peer_stage(k - 3)
+
+        table_stage(k)
+
+    @pl.loop(0, steps)
+    def _(k):
+        to_pair(k).wait_send()
+        to_peer(k).wait_send()
+        own_piece(k).wait()
+
+        @pl.loop(1, heads)
+        def _(i):
+            to_owner(k, i).wait_send()
+            from_owner(k, i).wait_recv()
+
+    for c in own_to_out:
+        c.wait()
+    for c in own_to_pair:
+        c.wait_send()
+        c.wait_recv()
+    for c in small_out:
+        c.wait()
+
+    @pl.loop(0, TABLE_PIECES)
+    def _(t):
+        t_peer(t).wait_send()
+        t_side(1, t).wait_send()
+        t_side(2, t).wait_send()
+        t_relay(t, False).wait_send()
+        for kind in range(4):
+            t_pair(kind, t).wait_send()
+            t_pair(kind, t).wait_recv()
+
+
+def back_kernel(
+    heads, steps, deltas, head_weight, spread, back_parts,
+    wv, e, x, db, acc, b1s, b1r, tot, b2,
+    w_sem, own_sem, d_send, d_recv, y_send, y_recv, p_send, p_recv, q_send, q_recv,
+    b_send, b_recv, c_send, c_recv, o_sem, z_sem,
+):
+    h, g = lax.axis_index("head"), lax.axis_index("client")
+    pair, peer = g ^ 1, g ^ 2
+    width = PIECE_ROWS * LANES
+    block_rows = steps * PIECE_ROWS
+    clients = db.shape[0] if db.ndim == 2 else db.shape[1]
+    group = clients // 4
+    each = clients // heads
+    units = acc.shape[0]
+
+    def place(c):
+        return (c & 1) * 2 + (c >> 1)
+
+    def w_copy(k):
+        return pltpu.make_async_copy(
+            head_weight.at[:, pl.ds(pl.multiple_of(k * width, width), width)], wv.at[k], w_sem.at[k]
+        )
+
+    def rows_of(head, k):
+        return pl.ds(pl.multiple_of(head * block_rows + k * PIECE_ROWS, PIECE_ROWS), PIECE_ROWS)
+
+    def own_piece(k):
+        return pltpu.make_async_copy(deltas.at[rows_of(h, k)], e.at[place(g), k, h], own_sem.at[k])
+
+    def to_holder(k, i):
+        other = lax.rem(h + i, heads)
+        return remote(
+            deltas.at[rows_of(other, k)], e.at[place(g), k, h],
+            d_send.at[k, other], d_recv.at[k, h], to_head(other),
+        )
+
+    def from_owner(k, i):
+        other = lax.rem(h + i, heads)
+        return remote(
+            deltas.at[rows_of(other, k)], e.at[place(g), k, other],
+            d_send.at[k, other], d_recv.at[k, other], to_head(other),
+        )
+
+    def to_peer(k):
+        ref = e.at[place(g), k]
+        return remote(ref, ref, y_send.at[k], y_recv.at[k], to_client(peer))
+
+    def from_peer(k):
+        ref = e.at[place(peer), k]
+        return remote(ref, ref, y_send.at[k], y_recv.at[k], to_client(peer))
+
+    def to_pair(k):
+        ref = e.at[place(g), k]
+        return remote(ref, ref, p_send.at[k], p_recv.at[k], to_client(pair))
+
+    def on_to_pair(k):
+        ref = e.at[place(peer), k]
+        return remote(ref, ref, q_send.at[k], q_recv.at[k], to_client(pair))
+
+    meet(heads, h, g)
+
+    @pl.loop(0, steps)
+    def _(k):
+        own_piece(k).start()
+
+        @pl.loop(1, heads)
+        def _(i):
+            to_holder(k, i).start()
+
+    @pl.loop(0, steps)
+    def _(k):
+        w_copy(k).start()
+
+    acc[...] = jnp.zeros_like(acc)
+
+    def spread_out(k):
+        return pltpu.make_async_copy(
+            db.at[k], spread.at[:, pl.ds(pl.multiple_of(k * width, width), width)], o_sem.at[k]
+        )
+
+    @pl.loop(0, steps + 2)
+    def _(k):
+        @pl.when(k < steps)
+        def _():
+            own_piece(k).wait()
+
+            @pl.loop(1, heads)
+            def _(i):
+                from_owner(k, i).wait_recv()
+
+            to_peer(k).start()
+            to_pair(k).start()
+
+        @pl.when((k >= 1) & (k < steps + 1))
+        def _():
+            from_peer(k - 1).wait_recv()
+            on_to_pair(k - 1).start()
+
+        @pl.when(k >= 2)
+        def _():
+            j = k - 2
+            to_pair(j).wait_recv()
+            on_to_pair(j).wait_recv()
+            for c in range(4):
+                x[c * group : (c + 1) * group] = e[c, j].astype(F32)
+            for q in range(PIECE_ROWS):
+                db[j, :, q * LANES : (q + 1) * LANES] = x[:, q, :].astype(BF16)
+            spread_out(j).start()
+            w_copy(j).wait()
+            acc[...] += lax.dot_general(
+                wv[j], db[j], (((1,), (1,)), ((), ())), preferred_element_type=F32
+            )
+
+    flat = acc[...].T
+    for j in range(heads):
+        for b in range(units // LANES):
+            b1s[j, b * each : (b + 1) * each, :] = flat[
+                j * each : (j + 1) * each, b * LANES : (b + 1) * LANES
+            ]
+
+    def part_to(i):
+        other = lax.rem(h + i, heads)
+        return remote(b1s.at[other], b1r.at[h], b_send.at[other], b_recv.at[h], to_head(other))
+
+    def part_from(i):
+        other = lax.rem(h + i, heads)
+        return remote(b1s.at[other], b1r.at[other], b_send.at[other], b_recv.at[other], to_head(other))
+
+    def sum_to(i):
+        other = lax.rem(h + i, heads)
+        return remote(tot, b2.at[h], c_send.at[other], c_recv.at[h], to_head(other))
+
+    def sum_from(i):
+        other = lax.rem(h + i, heads)
+        return remote(tot, b2.at[other], c_send.at[other], c_recv.at[other], to_head(other))
+
+    @pl.loop(1, heads)
+    def _(i):
+        part_to(i).start()
+
+    tot[...] = b1s[h]
+
+    @pl.loop(1, heads)
+    def _(i):
+        part_from(i).wait_recv()
+        tot[...] += b1r[lax.rem(h + i, heads)]
+
+    b2[h] = tot[...]
+
+    @pl.loop(1, heads)
+    def _(i):
+        sum_to(i).start()
+
+    @pl.loop(0, steps)
+    def _(k):
+        to_peer(k).wait_send()
+        to_pair(k).wait_send()
+        on_to_pair(k).wait_send()
+        spread_out(k).wait()
+
+        @pl.loop(1, heads)
+        def _(i):
+            to_holder(k, i).wait_send()
+
+    @pl.loop(1, heads)
+    def _(i):
+        part_to(i).wait_send()
+        sum_to(i).wait_send()
+        sum_from(i).wait_recv()
+
+    last = pltpu.make_async_copy(b2, back_parts, z_sem)
+    last.start()
+    last.wait()
+
+
+def grad_kernel(heads, hidden, spread, back_parts, preact, chosen, head_grad, in_grad, turned, hb):
+    clients, units = hidden.shape
+    each = clients // heads
+
+    @pl.when(pl.program_id(0) == 0)
+    def _():
+        turned[...] = hidden[...].astype(F32).T.astype(BF16)
+        for j in range(heads):
+            for b in range(units // LANES):
+                hb[j * each : (j + 1) * each, b * LANES : (b + 1) * LANES] = back_parts[
+                    j, b * each : (b + 1) * each, :
+                ]
+        masked = jnp.where(preact[...] > 0, hb[...], 0.0)
+        top = masked.astype(BF16)
+        rest = masked - top.astype(F32)
+        mid = rest.astype(BF16)
+        low = (rest - mid.astype(F32)).astype(BF16)
+        sel = chosen[...]
+        total = jnp.zeros(in_grad.shape, F32)
+        for term in (low, mid, top):
+            total += lax.dot_general(sel, term, (((0,), (0,)), ((), ())), preferred_element_type=F32)
+        in_grad[...] = total
+
+    head_grad[...] = jnp.dot(turned[...], spread[...], preferred_element_type=F32).astype(BF16)
+
+
 def local(
     client_ids, client_table, in_weight, in_bias, head_weight, tokens, labels, byte_table, out_table
 ):
-    head_count = lax.axis_size("head")
-    group_count = lax.axis_size("client")
-    per_device = tokens.shape[0]
-    byte_full, out_full = (
-        lax.all_gather(byte_table, "client", axis=1, tiled=True),
-        lax.all_gather(out_table, "client", axis=1, tiled=True),
-    )
+    heads = lax.axis_size("head")
+    groups = lax.axis_size("client")
+    assert groups == 4 and tokens.shape[0] == 1 and heads % 4 == 0
+    units, columns = head_weight.shape
+    clients = client_ids.shape[0]
+    embed = client_table.shape[1]
+    vocab, share = byte_table.shape
+    depth = share * groups
+    width = PIECE_ROWS * LANES
+    steps = columns // width
+    rows = heads * columns // LANES
+    group = clients // groups
+    each = clients // heads
+    part_rows = each * units // LANES
+    any_spec = pl.BlockSpec(memory_space=pl.ANY)
+    vmem_spec = pl.BlockSpec(memory_space=pltpu.VMEM)
+    dma = pltpu.SemaphoreType.DMA
+
+    ordered = client_ids.reshape(heads, 2, 2).transpose(2, 1, 0).reshape(clients, 1)
+    factors, tables, hidden, preact, chosen = pl.pallas_call(
+        functools.partial(forward_kernel, heads, steps),
+        name="forward",
+        out_shape=[
+            jax.ShapeDtypeStruct((rows, LANES), BF16),
+            jax.ShapeDtypeStruct((2, groups, vocab, share), BF16),
+            jax.ShapeDtypeStruct((clients, units), BF16),
+            jax.ShapeDtypeStruct((clients, units), F32),
+            jax.ShapeDtypeStruct((clients, embed), BF16),
+        ],
+        in_specs=[vmem_spec] + [any_spec] * 6,
+        out_specs=[any_spec] * 5,
+        scratch_shapes=[
+            pltpu.VMEM((steps, units, width), BF16),
+            pltpu.VMEM(client_table.shape, BF16),
+            pltpu.VMEM(in_weight.shape, BF16),
+            pltpu.VMEM((1, units), F32),
+            pltpu.VMEM((2, vocab, share), BF16),
+            pltpu.VMEM((clients, embed), BF16),
+            pltpu.VMEM((clients, units), F32),
+            pltpu.VMEM((clients, units), BF16),
+            pltpu.VMEM((steps, clients, PIECE_ROWS, LANES), F32),
+            pltpu.VMEM((steps, 2 * group, PIECE_ROWS, LANES), F32),
+            pltpu.VMEM((steps, group, PIECE_ROWS, LANES), F32),
+            pltpu.VMEM((steps, group, PIECE_ROWS, LANES), BF16),
+            pltpu.VMEM((steps, group, PIECE_ROWS, LANES), BF16),
+            pltpu.VMEM((steps, group, PIECE_ROWS, LANES), BF16),
+            dma((steps,)), dma((5,)), dma((3,)), dma((steps,)),
+            dma((steps,)), dma((steps,)), dma((steps,)), dma((steps,)),
+            dma((steps, heads)), dma((steps, heads)),
+            dma((2,)), dma((2,)), dma((4, TABLE_PIECES)), dma((4, TABLE_PIECES)),
+            dma((4, TABLE_PIECES)), dma((4, TABLE_PIECES)), dma((2,)),
+        ],
+        compiler_params=pltpu.CompilerParams(
+            collective_id=0, has_side_effects=True, vmem_limit_bytes=HIGH_VMEM
+        ),
+    )(ordered, client_table, in_weight, in_bias.reshape(1, units), head_weight, byte_table, out_table)
+
+    byte_full = tables[0].transpose(1, 0, 2).reshape(vocab, depth)
+    out_full = tables[1].transpose(1, 0, 2).reshape(vocab, depth)
     products = table_products(byte_full, out_full)
-    ordered = client_ids.reshape(head_count, group_count, per_device).transpose(1, 0, 2).reshape(-1)
-    chosen = client_table[ordered]
-    preact = jnp.dot(chosen, in_weight, preferred_element_type=jnp.float32) + in_bias
-    hidden = jnp.maximum(preact, 0.0).astype(jnp.bfloat16)
-    partial = jnp.dot(hidden, head_weight, preferred_element_type=jnp.float32).astype(jnp.bfloat16)
-    rows, columns = partial.shape
-    parts = lax.all_to_all(
-        partial.reshape(group_count, rows // group_count, columns), "client", split_axis=0, concat_axis=0
-    )
-    summed = jnp.sum(parts.astype(jnp.float32), 0)
-    owned = lax.all_to_all(
-        summed.astype(jnp.bfloat16), "head", split_axis=0, concat_axis=1, tiled=True
-    )
-    trained = [
-        train_client(owned[i], tokens[i], labels[i], byte_full, out_full, products)
-        for i in range(per_device)
-    ]
-    deltas = jnp.stack([t[0] for t in trained])
-    losses = jnp.stack([t[1] for t in trained])
-    returned = lax.all_to_all(deltas, "head", split_axis=1, concat_axis=0, tiled=True)
-    received = lax.all_gather(returned, "client", axis=0, tiled=True)
-    back = lax.dot_general(
-        received, head_weight, (((1,), (1,)), ((), ())), preferred_element_type=jnp.float32
-    )
-    back = lax.all_to_all(
-        back.reshape(head_count, rows // head_count, back.shape[1]), "head", split_axis=0, concat_axis=0
-    )
-    back = jnp.sum(back, 0)
-    back = lax.all_to_all(
-        jnp.broadcast_to(back[None], (head_count,) + back.shape), "head", split_axis=0, concat_axis=0
-    )
-    hidden_back = back.reshape(rows, back.shape[2])
-    grad_sum = lax.dot_general(
-        hidden, received, (((0,), (0,)), ((), ())), preferred_element_type=jnp.float32
-    )
-    masked = jnp.where(preact > 0, hidden_back, 0.0)
-    in_grad = lax.dot_general(
-        chosen.astype(jnp.float32),
-        masked,
-        (((0,), (0,)), ((), ())),
-        precision=FULL,
-    )
-    return (grad_sum.astype(jnp.bfloat16), in_grad, losses)
+    deltas, loss = train_client(factors.reshape(-1), tokens[0], labels[0], byte_full, out_full, products)
+    deltas = deltas.reshape(rows, LANES)
+
+    spread, back_parts = pl.pallas_call(
+        functools.partial(back_kernel, heads, steps),
+        name="back",
+        out_shape=[
+            jax.ShapeDtypeStruct((clients, columns), BF16),
+            jax.ShapeDtypeStruct((heads, part_rows, LANES), F32),
+        ],
+        in_specs=[any_spec] * 2,
+        out_specs=[any_spec] * 2,
+        scratch_shapes=[
+            pltpu.VMEM((steps, units, width), BF16),
+            pltpu.VMEM((groups, steps, heads, PIECE_ROWS, LANES), BF16),
+            pltpu.VMEM((clients, PIECE_ROWS, LANES), F32),
+            pltpu.VMEM((steps, clients, width), BF16),
+            pltpu.VMEM((units, clients), F32),
+            pltpu.VMEM((heads, part_rows, LANES), F32),
+            pltpu.VMEM((heads, part_rows, LANES), F32),
+            pltpu.VMEM((part_rows, LANES), F32),
+            pltpu.VMEM((heads, part_rows, LANES), F32),
+            dma((steps,)), dma((steps,)), dma((steps, heads)), dma((steps, heads)),
+            dma((steps,)), dma((steps,)), dma((steps,)), dma((steps,)), dma((steps,)), dma((steps,)),
+            dma((heads,)), dma((heads,)), dma((heads,)), dma((heads,)), dma((steps,)), dma,
+        ],
+        compiler_params=pltpu.CompilerParams(
+            collective_id=1, has_side_effects=True, vmem_limit_bytes=HIGH_VMEM
+        ),
+    )(deltas, head_weight)
+
+    block = 1024
+    fixed = lambda *shape: pl.BlockSpec(shape, lambda i: (0,) * len(shape))
+    head_grad, in_grad = pl.pallas_call(
+        functools.partial(grad_kernel, heads),
+        name="grad",
+        grid=(columns // block,),
+        out_shape=[
+            jax.ShapeDtypeStruct((units, columns), BF16),
+            jax.ShapeDtypeStruct((embed, units), F32),
+        ],
+        in_specs=[
+            fixed(clients, units),
+            pl.BlockSpec((clients, block), lambda i: (0, i)),
+            fixed(heads, part_rows, LANES),
+            fixed(clients, units),
+            fixed(clients, embed),
+        ],
+        out_specs=[pl.BlockSpec((units, block), lambda i: (0, i)), fixed(embed, units)],
+        scratch_shapes=[pltpu.VMEM((units, clients), BF16), pltpu.VMEM((clients, units), F32)],
+        compiler_params=pltpu.CompilerParams(vmem_limit_bytes=HIGH_VMEM),
+    )(hidden, spread, back_parts, preact, chosen)
+    return head_grad, in_grad, loss.reshape(1)
 
 
 def solution(mesh):

time: 179 us -> 141 us (0.79)
  Pallas kernels: 0 us -> 95.5 us
  matrix products: 68.6 us -> 23.5 us
  waiting for transfers between devices: 35.7 us -> 0 us
  blocking collectives: 26.8 us -> 0 us
  starting transfers between devices: 13.2 us -> 0 us
  between operations: 16.6 us -> 3.46 us
  other arithmetic: 4.36 us -> 2.35 us
  local copies, waits for them, and re-layouts: 13 us -> 14.9 us
    pallas_call x0 -> x3, Pallas kernels: none -> 95.5 us  [the longest x1 39.3 us: local(): pl.pallas_call(functools.partial(back_kernel, heads, steps), name='back',...]
    dot_general x5 -> x0, matrix products: 49.9 us -> none  [the longest x1 17.2 us: local(): lax.dot_general(received, head_weight, (((1,), (1,)), ((), ())), preferre...]
    all_to_all x2 -> x0, blocking collectives: 26.8 us -> none  [the longest x1 14.9 us: local(): lax.all_to_all(summed.astype(jnp.bfloat16), 'head', split_axis=0, concat_...]
    all_to_all x3 -> x0, waiting for transfers between devices: 19.1 us -> none  [the longest x1 13.6 us: local(): lax.all_to_all(partial.reshape(group_count, rows // group_count, columns)...]
    all_gather x3 -> x0, waiting for transfers between devices: 15.2 us -> none  [the longest x1 15.2 us: local(): received = lax.all_gather(returned, 'client', axis=0, tiled=True)]
    all_to_all x3 -> x0, starting transfers between devices: 13.2 us -> none  [the longest x1 5.51 us: local(): lax.all_to_all(back.reshape(head_count, rows // head_count, back.shape[1]...]
    transpose x1 -> x4, local copies, waits for them, and re-layouts: 0.08 us -> 9.36 us  [the longest x2 5.33 us: local(): byte_full = tables[0].transpose(1, 0, 2).reshape(vocab, depth)]
    dot_general x12, matrix products: 12.7 us -> 16.6 us  [exact(): lax.dot_general(x, y, (((over_x,), (over_y,)), ((), ())), preferred_eleme...]
  transfers between devices with their start and end apart: 6 -> 0, of which waited for: 3 -> 0; matrix products, arithmetic and copies ran while one was open for 25% -> 0% of each run, Pallas kernels for 0% -> 0%
where the time goes in v1:
time: 141 us; the launch traced here: 140 us
  Pallas kernels  95.5 us (68%)
  matrix products  23.5 us (17%)
  local copies, waits for them, and re-layouts  14.9 us (11%)
  between operations  3.46 us (2%)
  other arithmetic  2.35 us (2%)
    pallas_call x1, Pallas kernels, local(): pl.pallas_call(functools.partial(back_kernel, heads, steps), name='back',...  39.3 us
    pallas_call x1, Pallas kernels, local(): pl.pallas_call(functools.partial(forward_kernel, heads, steps), name='for...  37.6 us
    pallas_call x1, Pallas kernels, local(): pl.pallas_call(functools.partial(grad_kernel, heads), name='grad', grid=(...  18.5 us
    dot_general x12, matrix products, exact(): lax.dot_general(x, y, (((over_x,), (over_y,)), ((), ())), preferred_eleme...  16.6 us
    dot_general x26, matrix products, mm(): lax.dot_general(x, y, (((over_x,), (over_y,)), ((), ())), precision=FULL,...  6.94 us
    transpose x2, local copies, waits for them, and re-layouts, local(): byte_full = tables[0].transpose(1, 0, 2).reshape(vocab, depth)  5.33 us
    transpose x1, local copies, waits for them, and re-layouts, local(): out_full = tables[1].transpose(1, 0, 2).reshape(vocab, depth)  3.94 us

profile of v1, /device:TPU:0, one launch (start us, length us, event | category | flops | bytes accessed | tf_op | source)
XLA Modules:
  0.0 139.8 jit_solution(11853136836557385542)
XLA Ops:
  0.6 0.7 reshape.125
  1.5 0.7 reshape.136.ids
  2.2 37.6 %forward.1 = (bf16[1024,128]{1,0:T(8,128)(2,1)}, bf16[2,4,256,1024]{3,2,1,0:T(8,128)(2,1)}, bf16[32,1024]{1,0:T(8,128)(2,1)}, f32[32,1024]{1,0:T(8,128)}, bf16[32,256]{1,0:T(8,128)(2,1)}) custom-call(s32[32,1]{1,0:T(8,128)} %reshape.136.ids, bf16[128,256]{1,0:T(8,128)(2,1)} %client_table.1, bf16[256,1024]{1,0:T(8,128)(2,1)} %in_weight.1, ...), custom_call_target="tpu_custom_call" | custom-call | tf_op jit(solution)/shard_map/forward/pallas_call | solution.py:619
  39.8 3.1 %convolution_bitcast_fusion.1 = f32[256,256]{0,1:T(8,128)S(1)} fusion(bf16[2,4,256,1024]{3,2,1,0:T(8,128)(2,1)} %get-tuple-element.13), kind=kOutput, calls=%fused_computation.9 | convolution fusion | flops 536870912 | bytes 4456448 | tf_op jit(solution)/shard_map/dot_general | solution.py:28
  43.2 1.4 %convolution_bitcast_fusion = f32[256,256]{1,0:T(8,128)} fusion(bf16[2,4,256,1024]{3,2,1,0:T(8,128)(2,1)S(1)} %copy-done.1), kind=kOutput, calls=%fused_computation.8 | convolution fusion | flops 536870912 | bytes 2359296 | tf_op jit(solution)/shard_map/dot_general | solution.py:28
  44.7 0.7 fusion.73
  45.4 0.8 fusion.74
  46.2 3.8 %select_reduce_fusion = (f32[256]{0:T(256)S(1)}, f32[256,256]{0,1:T(8,128)}) fusion(bf16[2,4,256,1024]{3,2,1,0:T(8,128)(2,1)} %get-tuple-element.13), kind=kOutput, calls=%fused_computation.52 | convolution fusion | flops 537067264 | bytes 2360320 | tf_op jit(solution)/shard_map/dot_general | solution.py:28
  50.0 2.5 %slice_bitcast_fusion.1 = (bf16[256,4,1024]{2,0,1:T(8,128)(2,1)}, bf16[256,4,1024]{2,0,1:T(8,128)(2,1)}) fusion(bf16[2,4,256,1024]{3,2,1,0:T(8,128)(2,1)S(1)} %copy-done.2), kind=kLoop, calls=%fused_computation.3 | loop fusion | bytes 8388608 | tf_op jit(solution)/shard_map/transpose | solution.py:657
  52.5 2.8 %copy.17 = bf16[256,4,1024]{0,2,1:T(8,128)(2,1)S(1)} copy(bf16[256,4,1024]{2,0,1:T(8,128)(2,1)} %get-tuple-element.28) | data formatting | bytes 4194304 | tf_op jit(solution)/shard_map/transpose | solution.py:657
  55.9 1.0 fusion.77
  56.9 1.7 %reshape.129 = bf16[4096,16]{1,0:T(8,128)(2,1)S(1)} reshape(bf16[512,128]{1,0:T(8,128)(2,1)} %get-tuple-element.31) | data formatting | bytes 262144 | tf_op jit(solution)/shard_map/reshape | solution.py:81
  58.7 1.1 convolution_multiply_fusion.5
  60.1 3.9 %copy.18 = bf16[256,4,1024]{0,2,1:T(8,128)(2,1)} copy(bf16[256,4,1024]{2,0,1:T(8,128)(2,1)} %get-tuple-element.29) | data formatting | bytes 4194304 | tf_op jit(solution)/shard_map/transpose | solution.py:658
  64.1 2.0 %fusion.78 = f32[256,16]{0,1:T(8,128)S(1)} fusion(bf16[16,4096]{1,0:T(8,128)(2,1)S(1)} %reshape.130, bf16[256,4096]{0,1:T(8,128)(2,1)} %bitcast.83), kind=kOutput, calls=%fused_computation.145 | convolution fusion | flops 33554432 | bytes 2244608 | tf_op jit(solution)/shard_map/dot_general | solution.py:28
  66.6 0.9 multiply_reduce_fusion
  70.1 1.3 convolution_add_fusion.7
  76.2 0.7 fusion.35
  76.9 0.7 convolution_add_fusion.1
  77.7 0.7 fusion.31
  79.3 0.7 concatenate.21
  80.0 0.7 pad_maximum_fusion.deltas
  80.8 39.3 %back.1 = (bf16[32,16384]{1,0:T(8,128)(2,1)}, f32[8,32,128]{2,1,0:T(8,128)}) custom-call(bf16[1024,128]{1,0:T(8,128)(2,1)} %pad_maximum_fusion.deltas, bf16[1024,16384]{1,0:T(8,128)(2,1)} %head_weight.3), custom_call_target="tpu_custom_call" | custom-call | tf_op jit(solution)/shard_map/back/pallas_call | solution.py:663
  120.1 18.5 %grad.1 = (bf16[1024,16384]{1,0:T(8,128)(2,1)}, f32[256,1024]{1,0:T(8,128)}) custom-call(bf16[32,1024]{1,0:T(8,128)(2,1)} %get-tuple-element.12.hidden, bf16[32,16384]{1,0:T(8,128)(2,1)} %get-tuple-element.15.spread, f32[8,32,128]{2,1,0:T(8,128)} %get-tuple-element.16.back_parts, f32[32,1024]{1,0:T(8,128)} %get-tuple-element.17.preact, ...), custom_call_target="tpu_custom_call" | custom-call | tf_op jit(solution)/shard_map/grad/pallas_call | solution.py:693
  (69 shorter events, 8.7 us)
Async XLA Ops:
  39.8 3.5 %copy-start.1 = (bf16[2,4,256,1024]{3,2,1,0:T(8,128)(2,1)S(1)}, bf16[2,4,256,1024]{3,2,1,0:T(8,128)(2,1)}, u32[]{:S(2)}) copy-start(bf16[2,4,256,1024]{3,2,1,0:T(8,128)(2,1)} %get-tuple-element.13) | copy-start | bytes 12582916
  43.2 1.4 %copy-start.6 = (bf16[1024,128]{1,0:T(8,128)(2,1)S(1)}, bf16[1024,128]{1,0:T(8,128)(2,1)}, u32[]{:S(2)}) copy-start(bf16[1024,128]{1,0:T(8,128)(2,1)} %get-tuple-element.14) | copy-start | bytes 786436
  46.2 3.8 %copy-start.2 = (bf16[2,4,256,1024]{3,2,1,0:T(8,128)(2,1)S(1)}, bf16[2,4,256,1024]{3,2,1,0:T(8,128)(2,1)}, u32[]{:S(2)}) copy-start(bf16[2,4,256,1024]{3,2,1,0:T(8,128)(2,1)} %get-tuple-element.13) | copy-start | bytes 12582916
  50.0 5.3 %copy-start.9 = (f32[256]{0:T(256)}, f32[256]{0:T(256)S(1)}, u32[]{:S(2)}) copy-start(f32[256]{0:T(256)S(1)} %get-tuple-element.44) | copy-start | bytes 3076
  58.7 1.2 copy-start.4
  58.7 1.2 copy-start.7
  58.7 1.4 %copy-start.10 = (f32[256]{0:T(256)S(1)}, f32[256]{0:T(256)}, u32[]{:S(2)}) copy-start(f32[256]{0:T(256)} %copy-done.9) | copy-start | bytes 3076
  64.1 2.5 %copy-start.12 = (s32[1,256]{1,0:T(1,128)S(1)}, s32[1,256]{1,0:T(1,128)}, u32[]{:S(2)}) copy-start(s32[1,256]{1,0:T(1,128)} %param.15) | copy-start | bytes 3076
  64.1 2.5 %copy-start.13 = (s32[1,256]{1,0:T(1,128)S(1)}, s32[1,256]{1,0:T(1,128)}, u32[]{:S(2)}) copy-start(s32[1,256]{1,0:T(1,128)} %param.14) | copy-start | bytes 3076
  64.1 5.4 %copy-start.11 = (f32[256]{0:T(256)S(1)}, f32[256]{0:T(256)}, u32[]{:S(2)}) copy-start(f32[256]{0:T(256)} %copy-done.9) | copy-start | bytes 3076
  64.1 5.4 %copy-start.5 = (f32[256,16]{0,1:T(8,128)S(1)}, f32[256,16]{0,1:T(8,128)}, u32[]{:S(2)}) copy-start(f32[256,16]{0,1:T(8,128)} %fusion.77) | copy-start | bytes 49156
  66.1 6.4 %copy-start.8 = (f32[16,16]{1,0:T(8,128)S(1)}, f32[16,16]{1,0:T(8,128)}, u32[]{:S(2)}) copy-start(f32[16,16]{1,0:T(8,128)} %fusion.74) | copy-start | bytes 3076
  66.1 6.6 %copy-start.3 = (f32[256,256]{0,1:T(8,128)S(1)}, f32[256,256]{0,1:T(8,128)}, u32[]{:S(2)}) copy-start(f32[256,256]{0,1:T(8,128)} %get-tuple-element.45) | copy-start | bytes 786436
  71.4 4.8 %copy-start = (bf16[256,4,1024]{0,2,1:T(8,128)(2,1)S(1)}, bf16[256,4,1024]{0,2,1:T(8,128)(2,1)}, u32[]{:S(2)}) copy-start(bf16[256,4,1024]{0,2,1:T(8,128)(2,1)} %copy.18) | copy-start | bytes 6291460

commit v2 on v1

v2 whole, which is shorter than its diff:
```python
import functools

import jax
import jax.numpy as jnp
from jax import lax
from jax.experimental import pallas as pl
from jax.experimental.pallas import tpu as pltpu
from jax.sharding import PartitionSpec as P

EPSILON = 1e-06
learn_rate = 0.1
LANES = 128
PIECE_ROWS = 16
TABLE_PIECES = 8
HIGH_VMEM = 62 * 1024 * 1024
F32 = jnp.float32
BF16 = jnp.bfloat16


def split(x):
    top = x.astype(BF16)
    return top, (x - top.astype(F32)).astype(BF16)


def mm(x, y, over_x=1, over_y=0):
    (x_top, x_low), (y_top, y_low) = split(x), split(y)
    return (
        exact(x_top, y_low, over_x, over_y)
        + exact(x_low, y_top, over_x, over_y)
        + exact(x_top, y_top, over_x, over_y)
    )


def exact(x, y, over_x, over_y):
    return lax.dot_general(
        x, y, (((over_x,), (over_y,)), ((), ())), preferred_element_type=jnp.float32
    )


def inner_step(u, n_in, m_out, k_bb, gram_io, mean_in, pair_count, depth, scale):
    uk = mm(u, k_bb)
    z = gram_io + scale * mm(u, m_out, 1, 1)
    q = mean_in + jnp.sum(u * (2.0 * scale * n_in + (scale * scale) * uk), -1, keepdims=True) / depth
    r = lax.rsqrt(q + EPSILON)
    kappa = 4.0 / float(depth) ** 0.5
    logits = (kappa * r) * z
    top = jnp.max(logits, -1, keepdims=True)
    raised = jnp.exp(logits - top)
    total = jnp.sum(raised, -1, keepdims=True)
    row_count = jnp.sum(pair_count, -1, keepdims=True)
    loss = jnp.sum(
        row_count * (jnp.log(total) + top) - jnp.sum(pair_count * logits, -1, keepdims=True), 0, keepdims=True
    )
    slope = row_count * (raised / total) - pair_count
    dz = (kappa * r) * slope
    dr = kappa * jnp.sum(slope * z, -1, keepdims=True)
    e = dr * (-1.0 / depth) * (r * r * r)
    gu = scale * (mm(dz, m_out) + e * (n_in + scale * uk))
    w = mm(dz, u, 0, 0)
    x = e * u
    y = mm(u, x, 0, 0)
    return loss, gu, w, x, y


def table_products(tables):
    groups = tables.shape[1]

    def gram(left, right):
        total = exact(tables[left, 0], tables[right, 0], 1, 1)
        for c in range(1, groups):
            total += exact(tables[left, c], tables[right, c], 1, 1)
        return total

    return gram(0, 0), gram(0, 1), gram(1, 1)


def token_pairs(token_row, label_row, vocab):
    ids = lax.broadcasted_iota(jnp.int32, (vocab, token_row.shape[1]), 0)
    return exact(
        jnp.where(ids == token_row, 1.0, 0.0).astype(BF16),
        jnp.where(ids == label_row, 1.0, 0.0).astype(BF16),
        1,
        1,
    )


def train(factors, flat, spaced, b0, loss_ref, deltas, tables, grams, pair_count):
    gram_ii_ref, gram_io_ref, gram_oo_ref = grams
    groups, vocab, share = tables.shape[1:]
    depth = groups * share
    rows = factors.shape[0]
    rank = rows * LANES // (2 * depth)
    per_row = LANES // rank
    across = depth // LANES
    half = rows // 2
    scale = 1.0 / float(depth * rank) ** 0.5

    flat[...] = factors[...].astype(F32)
    lane = lax.broadcasted_iota(jnp.int32, (half // groups, per_row, LANES), 2)
    sub = lax.broadcasted_iota(jnp.int32, (half // groups, per_row, LANES), 1)
    here = lane // rank == sub
    for c in range(groups):
        q = half // groups
        wide = jnp.broadcast_to(flat[c * q : (c + 1) * q][:, None, :], (q, per_row, LANES))
        spaced[c * share : (c + 1) * share] = jnp.where(here, wide, 0.0).reshape(share, LANES).astype(BF16)
    for n in range(across):
        b0[:, n * LANES : (n + 1) * LANES] = flat[pl.ds(half + n, rank, stride=across), :].astype(BF16)

    def over_depth(f):
        total = f(0)
        for c in range(1, groups):
            total += f(c)
        return total

    cols = lambda c: slice(c * share, (c + 1) * share)
    folded = over_depth(lambda c: exact(tables[0, c], spaced[cols(c)], 1, 0))
    fold = jnp.where(
        lax.broadcasted_iota(jnp.int32, (LANES, rank), 0) % rank
        == lax.broadcasted_iota(jnp.int32, (LANES, rank), 1),
        1.0,
        0.0,
    )
    gram_ii, gram_io, gram_oo = gram_ii_ref[...], gram_io_ref[...], gram_oo_ref[...]
    diagonal = lax.broadcasted_iota(jnp.int32, (vocab, vocab), 0) == lax.broadcasted_iota(
        jnp.int32, (vocab, vocab), 1
    )
    mean_in = jnp.sum(jnp.where(diagonal, gram_ii, 0.0), -1, keepdims=True) / depth
    rn = lax.rsqrt(mean_in + EPSILON)
    u0 = rn * mm(folded, fold)
    n0 = over_depth(lambda c: exact(tables[0, c], b0[:, cols(c)], 1, 1))
    m0 = over_depth(lambda c: exact(tables[1, c], b0[:, cols(c)], 1, 1))
    k0 = exact(b0[...], b0[...], 1, 1)
    counts = pair_count[...]
    fixed = (gram_io, mean_in, counts, depth, scale)
    first_loss, gu0, w0, x0, y0 = inner_step(u0, n0, m0, k0, *fixed)
    loss_ref[...] = jnp.broadcast_to(first_loss, loss_ref.shape)
    rate = learn_rate * scale
    w0, x0, y0 = -rate * w0, -rate * x0, (-rate * scale) * y0
    u1 = u0 - learn_rate * rn * mm(gram_ii, rn * gu0)
    n1 = n0 + mm(gram_io, w0) + mm(gram_ii, x0) + mm(n0, y0)
    m1 = m0 + mm(gram_oo, w0) + mm(gram_io, x0, 0, 0) + mm(m0, y0)
    cross = k0 + mm(y0, k0, 0, 0) + mm(w0, m0, 0, 0) + mm(x0, n0, 0, 0)
    k1 = cross + mm(cross, y0) + mm(m1, w0, 0, 0) + mm(n1, x0, 0, 0)
    _, gu1, w1, x1, y1 = inner_step(u1, n1, m1, k1, *fixed)
    w1, x1, y1 = -rate * w1, -rate * x1, (-rate * scale) * y1
    ga = (-learn_rate) * rn * (gu0 + gu1)
    wf = w0 + w1 + mm(w0, y1)
    xf = x0 + x1 + mm(x0, y1)
    yf = y0 + y1 + mm(y0, y1)

    repeat = jnp.where(
        lax.broadcasted_iota(jnp.int32, (rank, LANES), 1) % rank
        == lax.broadcasted_iota(jnp.int32, (rank, LANES), 0),
        1.0,
        0.0,
    ).astype(BF16)
    ga_top, ga_low = (exact(t, repeat, 1, 0).astype(BF16) for t in split(ga))
    for c in range(groups):
        q = half // groups
        wide = exact(tables[0, c], ga_top, 0, 0) + exact(tables[0, c], ga_low, 0, 0)
        flat[c * q : (c + 1) * q] = jnp.sum(
            jnp.where(here, wide.reshape(q, per_row, LANES), 0.0), axis=1
        )
    parts = [jnp.concatenate([t.T for t in split(v)], 0) for v in (wf, xf, yf)]
    for c in range(groups):
        db = (
            exact(parts[0], tables[1, c], 1, 0)
            + exact(parts[1], tables[0, c], 1, 0)
            + exact(parts[2], b0[:, cols(c)], 1, 0)
        )
        db = db[:rank] + db[rank:]
        for n in range(share // LANES):
            flat[pl.ds(half + c * (share // LANES) + n, rank, stride=across), :] = db[
                :, n * LANES : (n + 1) * LANES
            ]
    deltas[...] = flat[...].astype(BF16)


def to_head(h):
    return {"head": h}


def to_client(g):
    return {"client": g}


def remote(src, dst, send, recv, device):
    return pltpu.make_async_remote_copy(
        src_ref=src,
        dst_ref=dst,
        send_sem=send,
        recv_sem=recv,
        device_id=device,
        device_id_type=pl.DeviceIdType.MESH,
    )


def enter(heads, h, g):
    sem = pltpu.get_barrier_semaphore()

    @pl.loop(1, heads)
    def _(i):
        pl.semaphore_signal(
            sem, inc=1, device_id=to_head(lax.rem(h + i, heads)), device_id_type=pl.DeviceIdType.MESH
        )

    for other in (g ^ 1, g ^ 2):
        pl.semaphore_signal(
            sem, inc=1, device_id=to_client(other), device_id_type=pl.DeviceIdType.MESH
        )


def await_others(heads):
    pl.semaphore_wait(pltpu.get_barrier_semaphore(), heads + 1)


def round_kernel(
    heads, steps, ids, token_row, label_row, client_table, in_weight, in_bias, head_weight, byte_table, out_table,
    spread, back_parts, hidden_out, preact_out, chosen_out, loss_out,
    wv, ct, iw, ib, tables, chosen_v, preact_v, hidden_v, s1, r1, k2, s2, r2, s3,
    factors, flat, spaced, b0, gram_ii, gram_io, gram_oo, pair_count, deltas,
    e, x, db, acc, b1s, b1r, tot, b2,
    w_sem, in_sem, out_sem, p_send, p_recv, y_send, y_recv, f_send, f_recv,
    t_own_send, t_own_recv, t_send, t_recv, t_pair_send, t_pair_recv,
    d_send, d_recv, e_send, e_recv, b_send, b_recv, c_send, c_recv, o_sem, z_sem,
):
    h, g = lax.axis_index("head"), lax.axis_index("client")
    core, far = g & 1, g >> 1
    pair, peer = g ^ 1, g ^ 2
    x_side, z_side = h ^ 1, h ^ 2
    clients, units = hidden_v.shape
    group = clients // 4
    each = clients // heads
    block_rows = steps * PIECE_ROWS
    width = PIECE_ROWS * LANES
    vocab = tables.shape[2]
    part = vocab // 4 // (TABLE_PIECES // 2)

    enter(heads, h, g)

    small = [
        pltpu.make_async_copy(client_table, ct, in_sem.at[0]),
        pltpu.make_async_copy(in_weight, iw, in_sem.at[1]),
        pltpu.make_async_copy(in_bias, ib, in_sem.at[2]),
        pltpu.make_async_copy(byte_table, tables.at[0, g], in_sem.at[3]),
        pltpu.make_async_copy(out_table, tables.at[1, g], in_sem.at[4]),
    ]
    for c in small:
        c.start()

    def w_copy(k):
        return pltpu.make_async_copy(
            head_weight.at[:, pl.ds(pl.multiple_of(k * width, width), width)], wv.at[k], w_sem.at[k]
        )

    @pl.loop(0, steps)
    def _(k):
        w_copy(k).start()

    for c in small:
        c.wait()
    population = lax.broadcasted_iota(jnp.int32, (clients, ct.shape[0]), 1)
    onehot = jnp.where(ids[...] == population, 1.0, 0.0).astype(BF16)
    chosen = jnp.dot(onehot, ct[...], preferred_element_type=F32).astype(BF16)
    chosen_v[...] = chosen
    preact = jnp.dot(chosen, iw[...], preferred_element_type=F32) + ib[...]
    preact_v[...] = preact
    hidden_v[...] = jnp.maximum(preact, 0.0).astype(BF16)

    def rows_of(head, k):
        return pl.ds(pl.multiple_of(head * block_rows + k * PIECE_ROWS, PIECE_ROWS), PIECE_ROWS)

    def piece(t, owner_head, col):
        table = lax.div(t, TABLE_PIECES // 2)
        row = lax.rem(owner_head, 4) * (vocab // 4) + lax.rem(t, TABLE_PIECES // 2) * part
        return tables.at[table, col, pl.ds(pl.multiple_of(row, part), part)]

    own_to_pair = [
        remote(tables.at[t, g], tables.at[t, g], t_own_send.at[t], t_own_recv.at[t], to_client(pair))
        for t in range(2)
    ]

    def t_peer(t):
        ref = piece(t, h, g)
        return remote(ref, ref, t_send.at[0, t], t_recv.at[0, t], to_client(peer))

    def t_side(kind, t):
        ref = piece(t, h, peer)
        return remote(ref, ref, t_send.at[kind, t], t_recv.at[kind, t], to_head((x_side, z_side)[kind - 1]))

    def t_relay(t, odd):
        ref = piece(t, x_side if odd else z_side, peer)
        return remote(ref, ref, t_send.at[3, t], t_recv.at[3, t], to_head(z_side if odd else x_side))

    def t_pair(kind, t):
        ref = piece(t, (h, x_side, z_side, h ^ 3)[kind], peer)
        return remote(ref, ref, t_pair_send.at[kind, t], t_pair_recv.at[kind, t], to_client(pair))

    def to_pair(k):
        return remote(
            s1.at[k, pl.ds((1 - core) * 2 * group, 2 * group)], r1.at[k],
            p_send.at[k], p_recv.at[k], to_client(pair),
        )

    def to_peer(k):
        return remote(s2.at[k], r2.at[k], y_send.at[k], y_recv.at[k], to_client(peer))

    def to_owner(k, i):
        other = lax.rem(h + i, heads)
        return remote(
            s3.at[k, other], factors.at[rows_of(h, k)],
            f_send.at[k, other], f_recv.at[k, h], to_head(other),
        )

    def from_holder(k, i):
        other = lax.rem(h + i, heads)
        return remote(
            s3.at[k, other], factors.at[rows_of(other, k)],
            f_send.at[k, other], f_recv.at[k, other], to_head(other),
        )

    small_out = [
        pltpu.make_async_copy(hidden_v, hidden_out, out_sem.at[0]),
        pltpu.make_async_copy(preact_v, preact_out, out_sem.at[1]),
        pltpu.make_async_copy(chosen_v, chosen_out, out_sem.at[2]),
    ]
    for c in small_out:
        c.start()

    def multiply_stage(k):
        w_copy(k).wait()
        for n in range(width // 512):
            out = jnp.dot(
                hidden_v[...], wv[k, :, n * 512 : (n + 1) * 512], preferred_element_type=F32
            )
            for q in range(4):
                s1[k, :, n * 4 + q, :] = out[:, q * LANES : (q + 1) * LANES]

    def pair_stage(k):
        to_pair(k).wait_recv()
        theirs = core * 2 * group + (1 - far) * group
        mine = core * 2 * group + far * group
        s2[k] = (s1[k, pl.ds(theirs, group)] + r1[k, pl.ds((1 - far) * group, group)]).astype(BF16)
        to_peer(k).start()
        k2[k] = s1[k, pl.ds(mine, group)] + r1[k, pl.ds(far * group, group)]

    def peer_stage(k):
        to_peer(k).wait_recv()
        s3[k] = (k2[k] + r2[k].astype(F32)).astype(BF16)

        @pl.loop(1, heads)
        def _(i):
            to_owner(k, i).start()

        factors[rows_of(h, k)] = s3[k, h]

    def table_stage(k):
        for kind, start in ((0, 2), (1, 4), (2, 6)):
            @pl.when((k >= start) & (k < start + TABLE_PIECES // 2))
            def _():
                for odd in (False, True):
                    t = 2 * (k - start) + (1 if odd else 0)
                    if kind == 0:
                        t_peer(t).wait_recv()
                        t_side(1, t).start()
                        t_side(2, t).start()
                        t_pair(0, t).start()
                    elif kind == 1:
                        t_side(1, t).wait_recv()
                        t_side(2, t).wait_recv()
                        t_relay(t, odd).start()
                        t_pair(1, t).start()
                        t_pair(2, t).start()
                    else:
                        t_relay(t, odd).wait_recv()
                        t_pair(3, t).start()

    await_others(heads)

    @pl.loop(0, TABLE_PIECES)
    def _(t):
        t_peer(t).start()

    for c in own_to_pair:
        c.start()

    PEER_LAG = 4

    @pl.loop(0, max(steps + PEER_LAG, TABLE_PIECES // 2 + 6))
    def _(k):
        @pl.when(k < steps)
        def _():
            multiply_stage(k)
            to_pair(k).start()

        @pl.when((k >= 1) & (k < steps + 1))
        def _():
            pair_stage(k - 1)

        @pl.when((k >= PEER_LAG) & (k < steps + PEER_LAG))
        def _():
            peer_stage(k - PEER_LAG)

        table_stage(k)

    for c in own_to_pair:
        c.wait_recv()

    @pl.loop(0, TABLE_PIECES)
    def _(t):
        for kind in range(4):
            t_pair(kind, t).wait_recv()

    gram_ii[...], gram_io[...], gram_oo[...] = table_products(tables)
    pair_count[...] = token_pairs(token_row[...], label_row[...], vocab)

    @pl.loop(0, steps)
    def _(k):
        @pl.loop(1, heads)
        def _(i):
            from_holder(k, i).wait_recv()

    train(factors, flat, spaced, b0, loss_out, deltas, tables, (gram_ii, gram_io, gram_oo), pair_count)

    def place(c):
        return (c & 1) * 2 + (c >> 1)

    def to_holder(k, i):
        other = lax.rem(h + i, heads)
        return remote(
            deltas.at[rows_of(other, k)], e.at[place(g), k, h],
            d_send.at[k, other], d_recv.at[k, h], to_head(other),
        )

    def from_owner(k, i):
        other = lax.rem(h + i, heads)
        return remote(
            deltas.at[rows_of(other, k)], e.at[place(g), k, other],
            d_send.at[k, other], d_recv.at[k, other], to_head(other),
        )

    def group_copy(kind, k, receive):
        sender = (peer, pair, pair)[kind] if receive else g
        ref = e.at[place((sender, sender, sender ^ 2)[kind]), k]
        return remote(ref, ref, e_send.at[kind, k], e_recv.at[kind, k], to_client((peer, pair, pair)[kind]))

    @pl.loop(0, steps)
    def _(k):
        @pl.loop(1, heads)
        def _(i):
            to_holder(k, i).start()

    acc[...] = jnp.zeros_like(acc)

    def spread_out(k):
        return pltpu.make_async_copy(
            db.at[k], spread.at[:, pl.ds(pl.multiple_of(k * width, width), width)], o_sem.at[k]
        )

    @pl.loop(0, steps + 2)
    def _(k):
        @pl.when(k < steps)
        def _():
            e[place(g), k, h] = deltas[rows_of(h, k)]

            @pl.loop(1, heads)
            def _(i):
                from_owner(k, i).wait_recv()

            group_copy(0, k, False).start()
            group_copy(1, k, False).start()

        @pl.when((k >= 1) & (k < steps + 1))
        def _():
            group_copy(0, k - 1, True).wait_recv()
            group_copy(2, k - 1, False).start()

        @pl.when(k >= 2)
        def _():
            j = k - 2
            group_copy(1, j, True).wait_recv()
            group_copy(2, j, True).wait_recv()
            for c in range(4):
                x[c * group : (c + 1) * group] = e[c, j].astype(F32)
            for q in range(PIECE_ROWS):
                db[j, :, q * LANES : (q + 1) * LANES] = x[:, q, :].astype(BF16)
            spread_out(j).start()
            acc[...] += lax.dot_general(
                wv[j], db[j], (((1,), (1,)), ((), ())), preferred_element_type=F32
            )

    turned = acc[...].T
    for j in range(heads):
        for b in range(units // LANES):
            b1s[j, b * each : (b + 1) * each, :] = turned[
                j * each : (j + 1) * each, b * LANES : (b + 1) * LANES
            ]

    def part_to(i):
        other = lax.rem(h + i, heads)
        return remote(b1s.at[other], b1r.at[h], b_send.at[other], b_recv.at[h], to_head(other))

    def part_from(i):
        other = lax.rem(h + i, heads)
        return remote(b1s.at[other], b1r.at[other], b_send.at[other], b_recv.at[other], to_head(other))

    def sum_to(i):
        other = lax.rem(h + i, heads)
        return remote(tot, b2.at[h], c_send.at[other], c_recv.at[h], to_head(other))

    def sum_from(i):
        other = lax.rem(h + i, heads)
        return remote(tot, b2.at[other], c_send.at[other], c_recv.at[other], to_head(other))

    @pl.loop(1, heads)
    def _(i):
        part_to(i).start()

    @pl.loop(0, steps)
    def _(k):
        to_pair(k).wait_send()
        to_peer(k).wait_send()
        spread_out(k).wait()
        for kind in range(3):
            group_copy(kind, k, False).wait_send()

        @pl.loop(1, heads)
        def _(i):
            to_owner(k, i).wait_send()
            to_holder(k, i).wait_send()

    for c in own_to_pair:
        c.wait_send()
    for c in small_out:
        c.wait()

    @pl.loop(0, TABLE_PIECES)
    def _(t):
        t_peer(t).wait_send()
        t_side(1, t).wait_send()
        t_side(2, t).wait_send()
        t_relay(t, False).wait_send()
        for kind in range(4):
            t_pair(kind, t).wait_send()

    tot[...] = b1s[h]

    @pl.loop(1, heads)
    def _(i):
        part_from(i).wait_recv()
        tot[...] += b1r[lax.rem(h + i, heads)]

    @pl.loop(1, heads)
    def _(i):
        sum_to(i).start()

    b2[h] = tot[...]

    @pl.loop(1, heads)
    def _(i):
        part_to(i).wait_send()
        sum_to(i).wait_send()
        sum_from(i).wait_recv()

    last = pltpu.make_async_copy(b2, back_parts, z_sem)
    last.start()
    last.wait()


def grad_kernel(heads, hidden, spread, back_parts, preact, chosen, head_grad, in_grad, turned, hb):
    clients, units = hidden.shape
    each = clients // heads

    @pl.when(pl.program_id(0) == 0)
    def _():
        turned[...] = hidden[...].astype(F32).T.astype(BF16)
        for j in range(heads):
            for b in range(units // LANES):
                hb[j * each : (j + 1) * each, b * LANES : (b + 1) * LANES] = back_parts[
                    j, b * each : (b + 1) * each, :
                ]
        masked = jnp.where(preact[...] > 0, hb[...], 0.0)
        top = masked.astype(BF16)
        rest = masked - top.astype(F32)
        mid = rest.astype(BF16)
        low = (rest - mid.astype(F32)).astype(BF16)
        sel = chosen[...]
        total = jnp.zeros(in_grad.shape, F32)
        for term in (low, mid, top):
            total += lax.dot_general(sel, term, (((0,), (0,)), ((), ())), preferred_element_type=F32)
        in_grad[...] = total

    head_grad[...] = jnp.dot(turned[...], spread[...], preferred_element_type=F32).astype(BF16)


def local(
    client_ids, client_table, in_weight, in_bias, head_weight, tokens, labels, byte_table, out_table
):
    heads = lax.axis_size("head")
    groups = lax.axis_size("client")
    assert groups == 4 and tokens.shape[0] == 1 and heads % 4 == 0
    units, columns = head_weight.shape
    clients = client_ids.shape[0]
    embed = client_table.shape[1]
    vocab, share = byte_table.shape
    depth = share * groups
    width = PIECE_ROWS * LANES
    steps = columns // width
    rows = heads * columns // LANES
    group = clients // groups
    each = clients // heads
    part_rows = each * units // LANES
    any_spec = pl.BlockSpec(memory_space=pl.ANY)
    vmem_spec = pl.BlockSpec(memory_space=pltpu.VMEM)
    dma = pltpu.SemaphoreType.DMA

    ordered = client_ids.reshape(heads, 2, 2).transpose(2, 1, 0).reshape(clients, 1)
    vmem = pltpu.VMEM
    spread, back_parts, hidden, preact, chosen, loss = pl.pallas_call(
        functools.partial(round_kernel, heads, steps),
        name="round",
        out_shape=[
            jax.ShapeDtypeStruct((clients, columns), BF16),
            jax.ShapeDtypeStruct((heads, part_rows, LANES), F32),
            jax.ShapeDtypeStruct((clients, units), BF16),
            jax.ShapeDtypeStruct((clients, units), F32),
            jax.ShapeDtypeStruct((clients, embed), BF16),
            jax.ShapeDtypeStruct((8, LANES), F32),
        ],
        in_specs=[vmem_spec] * 3 + [any_spec] * 6,
        out_specs=[any_spec] * 5 + [vmem_spec],
        scratch_shapes=[
            vmem((steps, units, width), BF16),
            vmem(client_table.shape, BF16),
            vmem(in_weight.shape, BF16),
            vmem((1, units), F32),
            vmem((2, groups, vocab, share), BF16),
            vmem((clients, embed), BF16),
            vmem((clients, units), F32),
            vmem((clients, units), BF16),
            vmem((steps, clients, PIECE_ROWS, LANES), F32),
            vmem((steps, 2 * group, PIECE_ROWS, LANES), F32),
            vmem((steps, group, PIECE_ROWS, LANES), F32),
            vmem((steps, group, PIECE_ROWS, LANES), BF16),
            vmem((steps, group, PIECE_ROWS, LANES), BF16),
            vmem((steps, group, PIECE_ROWS, LANES), BF16),
            vmem((rows, LANES), BF16),
            vmem((rows, LANES), F32),
            vmem((depth, LANES), BF16),
            vmem((rows * LANES // (2 * depth), depth), BF16),
            vmem((vocab, vocab), F32),
            vmem((vocab, vocab), F32),
            vmem((vocab, vocab), F32),
            vmem((vocab, vocab), F32),
            vmem((rows, LANES), BF16),
            vmem((groups, steps, heads, PIECE_ROWS, LANES), BF16),
            vmem((clients, PIECE_ROWS, LANES), F32),
            vmem((steps, clients, width), BF16),
            vmem((units, clients), F32),
            vmem((heads, part_rows, LANES), F32),
            vmem((heads, part_rows, LANES), F32),
            vmem((part_rows, LANES), F32),
            vmem((heads, part_rows, LANES), F32),
            dma((steps,)), dma((5,)), dma((3,)),
            dma((steps,)), dma((steps,)), dma((steps,)), dma((steps,)),
            dma((steps, heads)), dma((steps, heads)),
            dma((2,)), dma((2,)), dma((4, TABLE_PIECES)), dma((4, TABLE_PIECES)),
            dma((4, TABLE_PIECES)), dma((4, TABLE_PIECES)),
            dma((steps, heads)), dma((steps, heads)),
            dma((3, steps)), dma((3, steps)),
            dma((heads,)), dma((heads,)), dma((heads,)), dma((heads,)), dma((steps,)), dma,
        ],
        compiler_params=pltpu.CompilerParams(
            collective_id=0, has_side_effects=True, vmem_limit_bytes=HIGH_VMEM
        ),
    )(
        ordered, tokens, labels, client_table, in_weight, in_bias.reshape(1, units), head_weight,
        byte_table, out_table,
    )

    block = 2048
    fixed = lambda *shape: pl.BlockSpec(shape, lambda i: (0,) * len(shape))
    head_grad, in_grad = pl.pallas_call(
        functools.partial(grad_kernel, heads),
        name="grad",
        grid=(columns // block,),
        out_shape=[
            jax.ShapeDtypeStruct((units, columns), BF16),
            jax.ShapeDtypeStruct((embed, units), F32),
        ],
        in_specs=[
            fixed(clients, units),
            pl.BlockSpec((clients, block), lambda i: (0, i)),
            fixed(heads, part_rows, LANES),
            fixed(clients, units),
            fixed(clients, embed),
        ],
        out_specs=[pl.BlockSpec((units, block), lambda i: (0, i)), fixed(embed, units)],
        scratch_shapes=[pltpu.VMEM((units, clients), BF16), pltpu.VMEM((clients, units), F32)],
        compiler_params=pltpu.CompilerParams(vmem_limit_bytes=HIGH_VMEM),
    )(hidden, spread, back_parts, preact, chosen)
    return head_grad, in_grad, loss[0, :1] / tokens.shape[1]


def solution(mesh):
    placed = (
        P(),
        P(),
        P(None, "client"),
        P("client"),
        P("client", "head"),
        P(("head", "client"), None),
        P(("head", "client"), None),
        P(None, "client"),
        P(None, "client"),
    )
    return jax.shard_map(
        local,
        mesh=mesh,
        in_specs=placed,
        out_specs=(P("client", "head"), P(None, "client"), P(("head", "client"))),
        check_vma=False,
    )
```

time: 141 us -> 97.8 us (0.69)
  matrix products: 23.5 us -> 0 us
  local copies, waits for them, and re-layouts: 14.9 us -> 2.72 us
  Pallas kernels: 95.5 us -> 92.4 us
  other arithmetic: 2.35 us -> 0 us
    dot_general x38 -> x0, matrix products: 23.5 us -> none  [the longest x12 16.6 us: exact(): lax.dot_general(x, y, (((over_x,), (over_y,)), ((), ())), preferred_eleme...]
    transpose x3 -> x0, local copies, waits for them, and re-layouts: 9.27 us -> none  [the longest x2 5.33 us: local(): byte_full = tables[0].transpose(1, 0, 2).reshape(vocab, depth)]
    pallas_call x1, Pallas kernels: 18.5 us -> 16.2 us  [local(): pl.pallas_call(functools.partial(grad_kernel, heads), name='grad', grid=(...]
    reshape x2 -> x0, local copies, waits for them, and re-layouts: 1.81 us -> none  [the longest x1 1.75 us: train_client(): a0 = factor_row[:split_at].reshape(depth, rank)]
    pallas_call x2 -> x1, Pallas kernels: 76.9 us -> 76.2 us  [local(): pl.pallas_call(functools.partial(round_kernel, heads, steps), name='round...]
where the time goes in v2:
time: 97.8 us; the launch traced here: 97.5 us
  Pallas kernels  92.4 us (94%)
  local copies, waits for them, and re-layouts  2.72 us (3%)
  between operations  2.43 us (2%)
    pallas_call x1, Pallas kernels, local(): pl.pallas_call(functools.partial(round_kernel, heads, steps), name='round...  76.2 us
    pallas_call x1, Pallas kernels, local(): pl.pallas_call(functools.partial(grad_kernel, heads), name='grad', grid=(...  16.2 us

profile of v2, /device:TPU:0, one launch (start us, length us, event | category | flops | bytes accessed | tf_op | source)
XLA Modules:
  0.0 97.5 jit_solution(14084133938136717517)
XLA Ops:
  0.6 0.7 reshape.17
  1.4 0.1 copy.14
  1.5 0.7 reshape.20.ids
  2.2 76.2 %round.1 = (bf16[32,16384]{1,0:T(8,128)(2,1)}, f32[8,32,128]{2,1,0:T(8,128)}, bf16[32,1024]{1,0:T(8,128)(2,1)}, f32[32,1024]{1,0:T(8,128)}, bf16[32,256]{1,0:T(8,128)(2,1)}, /*index=5*/f32[8,128]{1,0:T(8,128)}) custom-call(s32[32,1]{1,0:T(8,128)} %reshape.20.ids, s32[1,256]{1,0:T(1,128)} %token_row.1, s32[1,256]{1,0:T(1,128)} %label_row.1, ...), custom_call_target="tpu_custom_call" | custom-call | tf_op jit(solution)/shard_map/round/pallas_call | solution.py:619
  78.4 1.2 %slice.3 = f32[1,1]{1,0:T(1,128)} slice(f32[8,128]{1,0:T(8,128)} %get-tuple-element.18), slice={[0:1], [0:1]} | slice | bytes 8 | tf_op jit(solution)/shard_map/slice | solution.py:702
  80.2 16.2 %grad.1 = (bf16[1024,16384]{1,0:T(8,128)(2,1)}, f32[256,1024]{1,0:T(8,128)}) custom-call(bf16[32,1024]{1,0:T(8,128)(2,1)} %get-tuple-element.11.hidden, bf16[32,16384]{1,0:T(8,128)(2,1)} %get-tuple-element.12.spread, f32[8,32,128]{2,1,0:T(8,128)} %get-tuple-element.13.back_parts, f32[32,1024]{1,0:T(8,128)} %get-tuple-element.14.preact, ...), custom_call_target="tpu_custom_call" | custom-call | tf_op jit(solution)/shard_map/grad/pallas_call | solution.py:683

commit v3 on v2

--- a/solution.py
+++ b/solution.py
@@ -10,6 +10,7 @@
 EPSILON = 1e-06
 learn_rate = 0.1
 LANES = 128
+TILE = 128
 PIECE_ROWS = 16
 TABLE_PIECES = 8
 HIGH_VMEM = 62 * 1024 * 1024
@@ -62,16 +63,9 @@
     return loss, gu, w, x, y
 
 
-def table_products(tables):
-    groups = tables.shape[1]
-
-    def gram(left, right):
-        total = exact(tables[left, 0], tables[right, 0], 1, 1)
-        for c in range(1, groups):
-            total += exact(tables[left, c], tables[right, c], 1, 1)
-        return total
-
-    return gram(0, 0), gram(0, 1), gram(1, 1)
+def add_grams(tables, grams, c):
+    for ref, left, right in zip(grams, (0, 0, 1), (0, 1, 1)):
+        ref[...] += exact(tables[left, c], tables[right, c], 1, 1)
 
 
 def token_pairs(token_row, label_row, vocab):
@@ -84,42 +78,57 @@
     )
 
 
-def train(factors, flat, spaced, b0, loss_ref, deltas, tables, grams, pair_count):
-    gram_ii_ref, gram_io_ref, gram_oo_ref = grams
-    groups, vocab, share = tables.shape[1:]
-    depth = groups * share
+def widen(factors, flat, spaced, b0, groups):
     rows = factors.shape[0]
-    rank = rows * LANES // (2 * depth)
+    share = spaced.shape[0] // groups
+    rank, depth = b0.shape
     per_row = LANES // rank
     across = depth // LANES
     half = rows // 2
-    scale = 1.0 / float(depth * rank) ** 0.5
-
+    q = half // groups
     flat[...] = factors[...].astype(F32)
-    lane = lax.broadcasted_iota(jnp.int32, (half // groups, per_row, LANES), 2)
-    sub = lax.broadcasted_iota(jnp.int32, (half // groups, per_row, LANES), 1)
-    here = lane // rank == sub
+    here = lanes_of_row(q, per_row, rank)
     for c in range(groups):
-        q = half // groups
         wide = jnp.broadcast_to(flat[c * q : (c + 1) * q][:, None, :], (q, per_row, LANES))
         spaced[c * share : (c + 1) * share] = jnp.where(here, wide, 0.0).reshape(share, LANES).astype(BF16)
     for n in range(across):
         b0[:, n * LANES : (n + 1) * LANES] = flat[pl.ds(half + n, rank, stride=across), :].astype(BF16)
 
-    def over_depth(f):
-        total = f(0)
-        for c in range(1, groups):
-            total += f(c)
-        return total
-
+
+def lanes_of_row(q, per_row, rank):
+    lane = lax.broadcasted_iota(jnp.int32, (q, per_row, LANES), 2)
+    sub = lax.broadcasted_iota(jnp.int32, (q, per_row, LANES), 1)
+    return lane // rank == sub
+
+
+def factor_products(tables, spaced, b0, c):
+    share = tables.shape[3]
+    here = pl.ds(pl.multiple_of(c * share, share), share)
+    return (
+        exact(tables[0, c], spaced[here], 1, 0),
+        exact(tables[0, c], b0[:, here], 1, 1),
+        exact(tables[1, c], b0[:, here], 1, 1),
+    )
+
+
+def train(products, flat, b0, loss_ref, deltas, tables, grams, pair_count):
+    gram_ii_ref, gram_io_ref, gram_oo_ref = grams
+    groups, vocab, share = tables.shape[1:]
+    depth = groups * share
+    rank = b0.shape[0]
+    per_row = LANES // rank
+    across = depth // LANES
+    half = flat.shape[0] // 2
+    scale = 1.0 / float(depth * rank) ** 0.5
+    here = lanes_of_row(half // groups, per_row, rank)
     cols = lambda c: slice(c * share, (c + 1) * share)
-    folded = over_depth(lambda c: exact(tables[0, c], spaced[cols(c)], 1, 0))
     fold = jnp.where(
         lax.broadcasted_iota(jnp.int32, (LANES, rank), 0) % rank
         == lax.broadcasted_iota(jnp.int32, (LANES, rank), 1),
         1.0,
         0.0,
     )
+    folded, n0, m0 = products
     gram_ii, gram_io, gram_oo = gram_ii_ref[...], gram_io_ref[...], gram_oo_ref[...]
     diagonal = lax.broadcasted_iota(jnp.int32, (vocab, vocab), 0) == lax.broadcasted_iota(
         jnp.int32, (vocab, vocab), 1
@@ -127,8 +136,6 @@
     mean_in = jnp.sum(jnp.where(diagonal, gram_ii, 0.0), -1, keepdims=True) / depth
     rn = lax.rsqrt(mean_in + EPSILON)
     u0 = rn * mm(folded, fold)
-    n0 = over_depth(lambda c: exact(tables[0, c], b0[:, cols(c)], 1, 1))
-    m0 = over_depth(lambda c: exact(tables[1, c], b0[:, cols(c)], 1, 1))
     k0 = exact(b0[...], b0[...], 1, 1)
     counts = pair_count[...]
     fixed = (gram_io, mean_in, counts, depth, scale)
@@ -259,11 +266,15 @@
 
     for c in small:
         c.wait()
-    population = lax.broadcasted_iota(jnp.int32, (clients, ct.shape[0]), 1)
-    onehot = jnp.where(ids[...] == population, 1.0, 0.0).astype(BF16)
-    chosen = jnp.dot(onehot, ct[...], preferred_element_type=F32).astype(BF16)
+    population = lax.broadcasted_iota(jnp.int32, (ct.shape[0], clients), 0)
+    onehot = jnp.where(population == ids[...][None, :], 1.0, 0.0).astype(BF16)
+    in_order = exact(onehot, ct[...], 0, 0).astype(BF16)
+    row = lax.broadcasted_iota(jnp.int32, (clients, clients), 0)
+    slot = lax.broadcasted_iota(jnp.int32, (clients, clients), 1)
+    slot_of_row = row % heads * 4 + row // heads % 2 * 2 + row // heads // 2
+    chosen = exact(jnp.where(slot == slot_of_row, 1.0, 0.0).astype(BF16), in_order, 1, 0).astype(BF16)
     chosen_v[...] = chosen
-    preact = jnp.dot(chosen, iw[...], preferred_element_type=F32) + ib[...]
+    preact = jnp.dot(chosen, iw[...], preferred_element_type=F32) + ib[...][None, :]
     preact_v[...] = preact
     hidden_v[...] = jnp.maximum(preact, 0.0).astype(BF16)
 
@@ -375,6 +386,10 @@
                         t_relay(t, odd).wait_recv()
                         t_pair(3, t).start()
 
+    grams = (gram_ii, gram_io, gram_oo)
+    for ref in grams:
+        ref[...] = jnp.zeros_like(ref)
+    pair_count[...] = token_pairs(token_row[...], label_row[...], vocab)
     await_others(heads)
 
     @pl.loop(0, TABLE_PIECES)
@@ -384,7 +399,7 @@
     for c in own_to_pair:
         c.start()
 
-    PEER_LAG = 4
+    PEER_LAG = 6
 
     @pl.loop(0, max(steps + PEER_LAG, TABLE_PIECES // 2 + 6))
     def _(k):
@@ -401,18 +416,16 @@
         def _():
             peer_stage(k - PEER_LAG)
 
+        @pl.when(k == steps)
+        def _():
+            for c in own_to_pair:
+                c.wait_recv()
+
+            @pl.loop(0, 2)
+            def _(i):
+                add_grams(tables, grams, g ^ i)
+
         table_stage(k)
-
-    for c in own_to_pair:
-        c.wait_recv()
-
-    @pl.loop(0, TABLE_PIECES)
-    def _(t):
-        for kind in range(4):
-            t_pair(kind, t).wait_recv()
-
-    gram_ii[...], gram_io[...], gram_oo[...] = table_products(tables)
-    pair_count[...] = token_pairs(token_row[...], label_row[...], vocab)
 
     @pl.loop(0, steps)
     def _(k):
@@ -420,7 +433,20 @@
         def _(i):
             from_holder(k, i).wait_recv()
 
-    train(factors, flat, spaced, b0, loss_out, deltas, tables, (gram_ii, gram_io, gram_oo), pair_count)
+    widen(factors, flat, spaced, b0, 4)
+    near = [factor_products(tables, spaced, b0, c) for c in (g, pair)]
+    add_grams(tables, grams, peer)
+    near.append(factor_products(tables, spaced, b0, peer))
+
+    @pl.loop(0, TABLE_PIECES)
+    def _(t):
+        for kind in range(4):
+            t_pair(kind, t).wait_recv()
+
+    add_grams(tables, grams, g ^ 3)
+    near.append(factor_products(tables, spaced, b0, g ^ 3))
+    products = [a + b + c + d for a, b, c, d in zip(*near)]
+    train(products, flat, b0, loss_out, deltas, tables, grams, pair_count)
 
     def place(c):
         return (c & 1) * 2 + (c >> 1)
@@ -457,7 +483,9 @@
             db.at[k], spread.at[:, pl.ds(pl.multiple_of(k * width, width), width)], o_sem.at[k]
         )
 
-    @pl.loop(0, steps + 2)
+    PEER_AFTER, PAIR_AFTER = 3, 5
+
+    @pl.loop(0, steps + PAIR_AFTER)
     def _(k):
         @pl.when(k < steps)
         def _():
@@ -470,20 +498,22 @@
             group_copy(0, k, False).start()
             group_copy(1, k, False).start()
 
-        @pl.when((k >= 1) & (k < steps + 1))
+        @pl.when((k >= PEER_AFTER) & (k < steps + PEER_AFTER))
         def _():
-            group_copy(0, k - 1, True).wait_recv()
-            group_copy(2, k - 1, False).start()
-
-        @pl.when(k >= 2)
+            group_copy(0, k - PEER_AFTER, True).wait_recv()
+            group_copy(2, k - PEER_AFTER, False).start()
+
+        @pl.when(k >= PAIR_AFTER)
         def _():
-            j = k - 2
+            j = k - PAIR_AFTER
             group_copy(1, j, True).wait_recv()
             group_copy(2, j, True).wait_recv()
+            apart = clients + 4
             for c in range(4):
-                x[c * group : (c + 1) * group] = e[c, j].astype(F32)
+                for i in range(group):
+                    x[pl.ds(c * group + i, PIECE_ROWS, stride=apart), :] = e[c, j, i].astype(F32)
             for q in range(PIECE_ROWS):
-                db[j, :, q * LANES : (q + 1) * LANES] = x[:, q, :].astype(BF16)
+                db[j, :, q * LANES : (q + 1) * LANES] = x[q * apart : q * apart + clients, :].astype(BF16)
             spread_out(j).start()
             acc[...] += lax.dot_general(
                 wv[j], db[j], (((1,), (1,)), ((), ())), preferred_element_type=F32
@@ -567,30 +597,65 @@
     last.wait()
 
 
-def grad_kernel(heads, hidden, spread, back_parts, preact, chosen, head_grad, in_grad, turned, hb):
+def grad_kernel(
+    heads, tokens, hidden, spread, back_parts, preact, chosen, loss,
+    head_grad, in_grad, losses, turned, hb, stage, ig, g_sem, i_sem,
+):
     clients, units = hidden.shape
     each = clients // heads
-
-    @pl.when(pl.program_id(0) == 0)
-    def _():
-        turned[...] = hidden[...].astype(F32).T.astype(BF16)
-        for j in range(heads):
-            for b in range(units // LANES):
-                hb[j * each : (j + 1) * each, b * LANES : (b + 1) * LANES] = back_parts[
-                    j, b * each : (b + 1) * each, :
-                ]
-        masked = jnp.where(preact[...] > 0, hb[...], 0.0)
-        top = masked.astype(BF16)
-        rest = masked - top.astype(F32)
-        mid = rest.astype(BF16)
-        low = (rest - mid.astype(F32)).astype(BF16)
-        sel = chosen[...]
-        total = jnp.zeros(in_grad.shape, F32)
-        for term in (low, mid, top):
-            total += lax.dot_general(sel, term, (((0,), (0,)), ((), ())), preferred_element_type=F32)
-        in_grad[...] = total
-
-    head_grad[...] = jnp.dot(turned[...], spread[...], preferred_element_type=F32).astype(BF16)
+    slots, _, block = stage.shape
+    steps = spread.shape[1] // block
+    turned[...] = hidden[...].astype(F32).T.astype(BF16)
+
+    def block_out(k):
+        return pltpu.make_async_copy(
+            stage.at[lax.rem(k, slots)],
+            head_grad.at[:, pl.ds(pl.multiple_of(k * block, block), block)],
+            g_sem.at[lax.rem(k, slots)],
+        )
+
+    def fill(first, last):
+        @pl.loop(first, last)
+        def _(k):
+            @pl.when(k >= slots)
+            def _():
+                block_out(k - slots).wait()
+
+            part = spread[:, pl.ds(pl.multiple_of(k * block, block), block)]
+            for m in range(0, units, TILE):
+                for n in range(0, block, 2 * TILE):
+                    stage[lax.rem(k, slots), m : m + TILE, n : n + 2 * TILE] = jnp.dot(
+                        turned[m : m + TILE], part[:, n : n + 2 * TILE], preferred_element_type=F32
+                    ).astype(BF16)
+            block_out(k).start()
+
+    early = min(slots, steps)
+    fill(0, early)
+    losses[0] = jnp.max(loss[...]) * (1.0 / tokens)
+    for j in range(heads):
+        for b in range(units // LANES):
+            hb[j * each : (j + 1) * each, b * LANES : (b + 1) * LANES] = back_parts[
+                j, b * each : (b + 1) * each, :
+            ]
+    masked = jnp.where(preact[...] > 0, hb[...], 0.0)
+    top = masked.astype(BF16)
+    rest = masked - top.astype(F32)
+    mid = rest.astype(BF16)
+    low = (rest - mid.astype(F32)).astype(BF16)
+    sel = chosen[...]
+    total = jnp.zeros(ig.shape, F32)
+    for term in (low, mid, top):
+        total += lax.dot_general(sel, term, (((0,), (0,)), ((), ())), preferred_element_type=F32)
+    ig[...] = total
+    ig_out = pltpu.make_async_copy(ig, in_grad, i_sem)
+    ig_out.start()
+    fill(early, steps)
+
+    @pl.loop(steps - early, steps)
+    def _(k):
+        block_out(k).wait()
+
+    ig_out.wait()
 
 
 def local(
@@ -614,7 +679,6 @@
     vmem_spec = pl.BlockSpec(memory_space=pltpu.VMEM)
     dma = pltpu.SemaphoreType.DMA
 
-    ordered = client_ids.reshape(heads, 2, 2).transpose(2, 1, 0).reshape(clients, 1)
     vmem = pltpu.VMEM
     spread, back_parts, hidden, preact, chosen, loss = pl.pallas_call(
         functools.partial(round_kernel, heads, steps),
@@ -633,7 +697,7 @@
             vmem((steps, units, width), BF16),
             vmem(client_table.shape, BF16),
             vmem(in_weight.shape, BF16),
-            vmem((1, units), F32),
+            vmem((units,), F32),
             vmem((2, groups, vocab, share), BF16),
             vmem((clients, embed), BF16),
             vmem((clients, units), F32),
@@ -654,7 +718,7 @@
             vmem((vocab, vocab), F32),
             vmem((rows, LANES), BF16),
             vmem((groups, steps, heads, PIECE_ROWS, LANES), BF16),
-            vmem((clients, PIECE_ROWS, LANES), F32),
+            vmem((PIECE_ROWS * (clients + 4), LANES), F32),
             vmem((steps, clients, width), BF16),
             vmem((units, clients), F32),
             vmem((heads, part_rows, LANES), F32),
@@ -674,32 +738,33 @@
             collective_id=0, has_side_effects=True, vmem_limit_bytes=HIGH_VMEM
         ),
     )(
-        ordered, tokens, labels, client_table, in_weight, in_bias.reshape(1, units), head_weight,
+        client_ids, tokens, labels, client_table, in_weight, in_bias, head_weight,
         byte_table, out_table,
     )
 
-    block = 2048
-    fixed = lambda *shape: pl.BlockSpec(shape, lambda i: (0,) * len(shape))
-    head_grad, in_grad = pl.pallas_call(
-        functools.partial(grad_kernel, heads),
+    block = min(1024, columns)
+    slots = 4
+    head_grad, in_grad, losses = pl.pallas_call(
+        functools.partial(grad_kernel, heads, tokens.shape[1]),
         name="grad",
-        grid=(columns // block,),
         out_shape=[
             jax.ShapeDtypeStruct((units, columns), BF16),
             jax.ShapeDtypeStruct((embed, units), F32),
+            jax.ShapeDtypeStruct((1,), F32),
         ],
-        in_specs=[
-            fixed(clients, units),
-            pl.BlockSpec((clients, block), lambda i: (0, i)),
-            fixed(heads, part_rows, LANES),
-            fixed(clients, units),
-            fixed(clients, embed),
+        in_specs=[vmem_spec] * 6,
+        out_specs=[any_spec, any_spec, pl.BlockSpec(memory_space=pltpu.SMEM)],
+        scratch_shapes=[
+            vmem((units, clients), BF16),
+            vmem((clients, units), F32),
+            vmem((slots, units, block), BF16),
+            vmem((embed, units), F32),
+            dma((slots,)),
+            dma,
         ],
-        out_specs=[pl.BlockSpec((units, block), lambda i: (0, i)), fixed(embed, units)],
-        scratch_shapes=[pltpu.VMEM((units, clients), BF16), pltpu.VMEM((clients, units), F32)],
         compiler_params=pltpu.CompilerParams(vmem_limit_bytes=HIGH_VMEM),
-    )(hidden, spread, back_parts, preact, chosen)
-    return head_grad, in_grad, loss[0, :1] / tokens.shape[1]
+    )(hidden, spread, back_parts, preact, chosen, loss)
+    return head_grad, in_grad, losses
 
 
 def solution(mesh):

time: 97.8 us -> 86.7 us (0.89)
  Pallas kernels: 92.4 us -> 85.9 us
  local copies, waits for them, and re-layouts: 2.72 us -> 0 us
  between operations: 2.43 us -> 0.64 us
    pallas_call x1, Pallas kernels: 76.2 us -> 71.1 us  [local(): pl.pallas_call(functools.partial(round_kernel, heads, steps), name='round...]
    reshape x2 -> x0, local copies, waits for them, and re-layouts: 1.44 us -> none  [local(): client_ids.reshape(heads, 2, 2).transpose(2, 1, 0).reshape(clients, 1)]
    pallas_call x1, Pallas kernels: 16.2 us -> 14.9 us  [local(): pl.pallas_call(functools.partial(grad_kernel, heads, tokens.shape[1]), na...]
    slice x1 -> x0, local copies, waits for them, and re-layouts: 1.18 us -> none  [local(): return (head_grad, in_grad, loss[0, :1] / tokens.shape[1])]
where the time goes in v3:
time: 86.7 us; the launch traced here: 86.6 us
  Pallas kernels  85.9 us (99%)
    pallas_call x1, Pallas kernels, local(): pl.pallas_call(functools.partial(round_kernel, heads, steps), name='round...  71.1 us
    pallas_call x1, Pallas kernels, local(): pl.pallas_call(functools.partial(grad_kernel, heads, tokens.shape[1]), na...  14.9 us

profile of v3, /device:TPU:0, one launch (start us, length us, event | category | flops | bytes accessed | tf_op | source)
XLA Modules:
  0.0 86.6 jit_solution(3223752011669752108)
XLA Ops:
  0.6 71.1 %round.1 = (bf16[32,16384]{1,0:T(8,128)(2,1)}, f32[8,32,128]{2,1,0:T(8,128)}, bf16[32,1024]{1,0:T(8,128)(2,1)}, f32[32,1024]{1,0:T(8,128)}, bf16[32,256]{1,0:T(8,128)(2,1)}, /*index=5*/f32[8,128]{1,0:T(8,128)}) custom-call(s32[32]{0:T(128)} %ids.1, s32[1,256]{1,0:T(1,128)} %token_row.1, s32[1,256]{1,0:T(1,128)} %label_row.1, bf16[128,256]{1,0:T(8,128)(2,1)} %client_table.1, ...), custom_call_target="tpu_custom_call" | custom-call | tf_op jit(solution)/shard_map/round/pallas_call | solution.py:683
  71.7 14.9 %grad.1 = (bf16[1024,16384]{1,0:T(8,128)(2,1)}, f32[256,1024]{1,0:T(8,128)}, f32[1]{0:T(128)}) custom-call(bf16[32,1024]{1,0:T(8,128)(2,1)} %get-tuple-element.9.hidden, bf16[32,16384]{1,0:T(8,128)(2,1)} %get-tuple-element.10.spread, f32[8,32,128]{2,1,0:T(8,128)} %get-tuple-element.11.back_parts, f32[32,1024]{1,0:T(8,128)} %get-tuple-element.12.preact, ...), custom_call_target="tpu_custom_call" | custom-call | tf_op jit(solution)/shard_map/grad/pallas_call | solution.py:747

commit v4 on v3

--- a/solution.py
+++ b/solution.py
@@ -416,16 +416,14 @@
         def _():
             peer_stage(k - PEER_LAG)
 
-        @pl.when(k == steps)
-        def _():
-            for c in own_to_pair:
-                c.wait_recv()
-
-            @pl.loop(0, 2)
-            def _(i):
-                add_grams(tables, grams, g ^ i)
-
         table_stage(k)
+
+    for c in own_to_pair:
+        c.wait_recv()
+
+    @pl.loop(0, 3)
+    def _(i):
+        add_grams(tables, grams, g ^ i)
 
     @pl.loop(0, steps)
     def _(k):
@@ -435,7 +433,6 @@
 
     widen(factors, flat, spaced, b0, 4)
     near = [factor_products(tables, spaced, b0, c) for c in (g, pair)]
-    add_grams(tables, grams, peer)
     near.append(factor_products(tables, spaced, b0, peer))
 
     @pl.loop(0, TABLE_PIECES)

time: 86.7 us -> 85.9 us (level)
  no operation moved by 1% of the time
where the time goes in v4:
time: 85.9 us; the launch traced here: 85.7 us
  Pallas kernels  85.1 us (99%)
    pallas_call x1, Pallas kernels, local(): pl.pallas_call(functools.partial(round_kernel, heads, steps), name='round...  70.2 us
    pallas_call x1, Pallas kernels, local(): pl.pallas_call(functools.partial(grad_kernel, heads, tokens.shape[1]), na...  14.9 us

profile of v4, /device:TPU:0, one launch (start us, length us, event | category | flops | bytes accessed | tf_op | source)
XLA Modules:
  0.0 85.7 jit_solution(10672257320748186316)
XLA Ops:
  0.6 70.2 %round.1 = (bf16[32,16384]{1,0:T(8,128)(2,1)}, f32[8,32,128]{2,1,0:T(8,128)}, bf16[32,1024]{1,0:T(8,128)(2,1)}, f32[32,1024]{1,0:T(8,128)}, bf16[32,256]{1,0:T(8,128)(2,1)}, /*index=5*/f32[8,128]{1,0:T(8,128)}) custom-call(s32[32]{0:T(128)} %ids.1, s32[1,256]{1,0:T(1,128)} %token_row.1, s32[1,256]{1,0:T(1,128)} %label_row.1, bf16[128,256]{1,0:T(8,128)(2,1)} %client_table.1, ...), custom_call_target="tpu_custom_call" | custom-call | tf_op jit(solution)/shard_map/round/pallas_call | solution.py:680
  70.9 14.9 %grad.1 = (bf16[1024,16384]{1,0:T(8,128)(2,1)}, f32[256,1024]{1,0:T(8,128)}, f32[1]{0:T(128)}) custom-call(bf16[32,1024]{1,0:T(8,128)(2,1)} %get-tuple-element.9.hidden, bf16[32,16384]{1,0:T(8,128)(2,1)} %get-tuple-element.10.spread, f32[8,32,128]{2,1,0:T(8,128)} %get-tuple-element.11.back_parts, f32[32,1024]{1,0:T(8,128)} %get-tuple-element.12.preact, ...), custom_call_target="tpu_custom_call" | custom-call | tf_op jit(solution)/shard_map/grad/pallas_call | solution.py:744
